TPU v7x, 128 devices: a whole 4x4x4 slice. The times are simulated.
128 devices in a mesh: tp: 16 (over z, y), dp: 8 (over x, core).
Axes of the slice: x: 4, y: 4, z: 4, core: 2. Of those that a mesh axis runs over, the one named last changes fastest.
Arguments:
- hidden: bfloat16 [8, 4096, 768], P('dp')
- residual: float32 [8, 4096, 768], P('dp')
- targets: int32 [8, 4096], P('dp')
- embedding: bfloat16 [50288, 768], P('tp')
- norm_w: float32 [768], replicated
Outputs:
- output 1: float32 [], replicated
- output 2: float32 [8, 4096, 768], P('dp')
- output 3: float32 [50288, 768], P('tp')
- output 4: float32 [768], replicated
All inputs are finite; a program needn't handle non-finite values.
Results may differ from a plain program's by a relative error of at most 0.001.
Values sent between devices are 32-bit elements.
A program may use at most 1 GiB of HBM per device.

v0:
```python
import jax
import jax.numpy as jnp
from jax import lax
from jax.sharding import PartitionSpec as P

NORM_EPS = 1e-5


def solution(mesh):
    def program(hidden, residual, targets, embedding, norm_w):
        inv_n = 1.0 / (hidden.shape[0] * hidden.shape[1])

        def local_part(hid_loc, res_loc, tgt_loc, emb_loc, norm_vec):
            n_batch, n_seq, d_model = hid_loc.shape
            n_rows = n_batch * n_seq
            vocab_loc = emb_loc.shape[0]
            resid = (res_loc + hid_loc.astype(jnp.float32)).reshape(n_rows, d_model)
            tgt_rows = tgt_loc.reshape(n_rows)
            inv_rms = lax.rsqrt(jnp.mean(resid * resid, axis=-1, keepdims=True) + NORM_EPS)
            scaled_r = resid * inv_rms
            h_act = (scaled_r * norm_vec).astype(jnp.bfloat16)
            logits = jnp.einsum('td,vd->tv', h_act, emb_loc, preferred_element_type=jnp.float32)
            row_max = lax.pmax(jnp.max(logits, axis=-1, keepdims=True), 'tp')
            exp_shift = jnp.exp(logits - row_max)
            local_ids = tgt_rows - lax.axis_index('tp') * vocab_loc
            is_target = lax.broadcasted_iota(jnp.int32, (1, vocab_loc), 1) == local_ids[:, None]
            part_stats = jnp.stack([jnp.sum(exp_shift, axis=-1), jnp.sum(jnp.where(is_target, logits, 0.0), axis=-1)], axis=-1)
            tok_stats = lax.psum(part_stats, 'tp')
            sum_exp = tok_stats[:, 0:1]
            loss_part = jnp.sum(row_max[:, 0] + jnp.log(tok_stats[:, 0]) - tok_stats[:, 1]) * inv_n
            prob_rows = exp_shift / sum_exp
            dlogits = (jnp.where(is_target, prob_rows - 1.0, prob_rows) * inv_n).astype(jnp.bfloat16)
            grad_h = lax.psum(jnp.einsum('tv,vd->td', dlogits, emb_loc, preferred_element_type=jnp.float32), 'tp')
            grad_emb = lax.psum(jnp.einsum('tv,td->vd', dlogits, h_act, preferred_element_type=jnp.float32), 'dp')
            grad_scaled = grad_h * norm_vec
            grad_r = inv_rms * (grad_scaled - scaled_r * jnp.mean(grad_scaled * scaled_r, axis=-1, keepdims=True))
            grad_w, loss_mean = lax.psum((jnp.sum(grad_h * scaled_r, axis=0), loss_part), 'dp')
            return loss_mean, grad_r.reshape(n_batch, n_seq, d_model), grad_emb, grad_w

        sharded = jax.shard_map(
            local_part, mesh=mesh,
            in_specs=(P('dp', None, None), P('dp', None, None), P('dp', None), P('tp', None), P(None)),
            out_specs=(P(), P('dp', None, None), P('tp', None), P(None)),
            check_vma=False)
        return sharded(hidden, residual, targets, embedding, norm_w)

    return program
```

profile of v0, /device:TPU:1, one launch (start us, length us, event | category | flops | bytes accessed | tf_op | source)
XLA Modules:
  0.0 582.6 jit_solution(5448990364292687181)
XLA Ops:
  7.2 0.0 all-reduce.4.cloned.1.call-start
  7.2 0.0 copy-start
  7.2 12.3 %fusion.3 = (f32[4096]{0:T(1024)S(1)}, f32[1,4096,768]{2,1,0:T(8,128)}) fusion(f32[1,4096,768]{2,1,0:T(8,128)} %param.6, bf16[1,4096,768]{2,1,0:T(8,128)(2,1)} %param.5), kind=kLoop, calls=%fused_computation.9 | loop fusion | flops 12578816 | bytes 31473664 | tf_op jit(solution)/shard_map/reduce_sum | solution.py:19
  19.5 0.0 copy-done
  19.5 0.0 copy-start.1
  19.5 32.1 %fusion.7 = (f32[4096]{0:T(1024)S(1)}, f32[4096,3143]{0,1:T(8,128)}) fusion(bf16[3143,768]{1,0:T(8,128)(2,1)} %param.8, f32[1,4096,768]{2,1,0:T(8,128)} %get-tuple-element.11, f32[768]{0:T(1024)S(1)} %copy-done, f32[4096]{0:T(1024)S(1)} %add_rsqrt_fusion), kind=kOutput, calls=%fused_computation.23 | convolution fusion | flops 19796353024 | bytes 68941312 | tf_op jit(solution)/shard_map/td,vd->tv/dot_general | solution.py:22
  51.6 62.5 %pmax.7 = f32[4096]{0:T(1024)S(1)} all-reduce(f32[4096]{0:T(1024)S(1)} %get-tuple-element.14), channel_id=1, replica_groups=mesh['tp'=16,'dp'=8] {'tp'}, use_global_device_ids=true, to_apply=%region_2.0 | all-reduce | flops 4096 | bytes 32768 | tf_op jit(solution)/shard_map/pmax | solution.py:23
  114.1 0.0 copy-done.1
  114.1 22.5 %fusion.2 = (f32[4096]{0:T(1024)S(1)}, f32[4096]{0:T(1024)S(1)}) fusion(f32[4096,3143]{0,1:T(8,128)} %get-tuple-element.15, f32[4096]{0:T(1024)S(1)} %pmax.7, s32[4096]{0:T(1024)S(1)} %bitcast.28), kind=kLoop, calls=%fused_computation.6 | loop fusion | flops 64360448 | bytes 51560448 | tf_op jit(solution)/shard_map/reduce_sum | solution.py:27
  136.7 55.9 %psum.35 = f32[4096,2]{0,1:T(2,128)S(1)} all-reduce(f32[4096,2]{0,1:T(2,128)S(1)} %pad_maximum_fusion), channel_id=1, replica_groups=mesh['tp'=16,'dp'=8] {'tp'}, use_global_device_ids=true, to_apply=%region_5.6 | all-reduce | flops 8192 | bytes 65536 | tf_op jit(solution)/shard_map/psum | solution.py:28
  192.6 26.5 %fusion.1 = bf16[4096,3143]{0,1:T(8,128)(2,1)} fusion(f32[4096,3143]{0,1:T(8,128)} %get-tuple-element.15, f32[4096]{0:T(1024)S(1)} %bitcast.30, s32[4096]{0:T(1024)S(1)} %bitcast.29, f32[4096]{0:T(1024)S(1)} %pmax.7), kind=kLoop, calls=%fused_computation.2 | loop fusion | flops 90116096 | bytes 77291520 | tf_op jit(solution)/shard_map/convert_element_type | solution.py:32
  219.1 27.6 %fusion.8 = f32[4096,768]{1,0:T(8,128)} fusion(bf16[4096,3143]{0,1:T(8,128)(2,1)} %fusion.1, bf16[3143,768]{1,0:T(8,128)(2,1)} %param.8), kind=kOutput, calls=%fused_computation.24 | convolution fusion | flops 19774046208 | bytes 43158016 | tf_op jit(solution)/shard_map/tv,vd->td/dot_general | solution.py:33
  246.7 0.0 all-reduce.4.cloned.1.call-update
  246.7 0.2 all-reduce.6.cloned.1.call-start
  246.9 29.2 %fusion.4 = f32[3143,768]{1,0:T(8,128)} fusion(bf16[4096,3143]{0,1:T(8,128)(2,1)} %fusion.1, f32[1,4096,768]{2,1,0:T(8,128)} %get-tuple-element.11, f32[768]{0:T(1024)S(1)} %copy-done, f32[4096]{0:T(1024)S(1)} %add_rsqrt_fusion), kind=kOutput, calls=%fused_computation.20 | convolution fusion | flops 19783483392 | bytes 48005120 | tf_op jit(solution)/shard_map/tv,td->vd/dot_general | solution.py:34
  276.1 0.0 all-reduce.6.cloned.1.call-update
  276.1 0.6 subtract_reduce_fusion
  277.4 171.4 %all-reduce.4.cloned.1.call-done = f32[4096,768]{1,0:T(8,128)} async-done(((f32[4096,768]{1,0:T(8,128)}), f32[4096,768]{1,0:T(8,128)}) %all-reduce.4.cloned.1.call-update) | async-done | bytes 12582928 | tf_op jit(solution)/shard_map/psum | solution.py:33
  448.8 9.3 %multiply_reduce_fusion = (f32[768]{0:T(1024)S(1)}, f32[4096]{0:T(1024)S(1)}) fusion(f32[4096,768]{1,0:T(8,128)} %all-reduce.4.cloned.1.call-done, f32[1,4096,768]{2,1,0:T(8,128)} %get-tuple-element.11, f32[4096]{0:T(1024)S(1)} %add_rsqrt_fusion, f32[768]{0:T(1024)S(1)} %copy-done), kind=kLoop, calls=%fused_computation.10 | loop fusion | flops 18869504 | bytes 25204736 | tf_op jit(solution)/shard_map/reduce_sum | solution.py:37
  458.1 13.7 %all-reduce = (f32[]{:T(128)}, f32[768]{0:T(1024)}) all-reduce(f32[]{:T(128)S(6)} %mul.63, f32[768]{0:T(1024)S(1)} %get-tuple-element.6), channel_id=1, replica_groups=mesh['tp'=16,'dp'=8] {'dp'}, use_global_device_ids=true, to_apply=%region_7.8 | all-reduce | flops 769 | bytes 6152 | tf_op jit(solution)/shard_map/psum | solution.py:37
  471.9 14.2 %multiply_bitcast_fusion = f32[1,4096,768]{2,1,0:T(8,128)} fusion(f32[4096,768]{1,0:T(8,128)} %all-reduce.4.cloned.1.call-done, f32[1,4096,768]{2,1,0:T(8,128)} %get-tuple-element.11, f32[4096]{0:T(1024)S(1)} %broadcast_multiply_fusion, f32[768]{0:T(1024)S(1)} %copy-done, f32[4096]{0:T(1024)S(1)} %add_rsqrt_fusion), kind=kLoop, calls=%fused_computation.11 | loop fusion | flops 15728640 | bytes 37784576 | tf_op jit(solution)/shard_map/reshape | solution.py:38
  486.1 81.5 %all-reduce.6.cloned.1.call-done = f32[3143,768]{1,0:T(8,128)} async-done(((f32[3143,768]{1,0:T(8,128)}), f32[3143,768]{1,0:T(8,128)}) %all-reduce.6.cloned.1.call-update) | async-done | bytes 9655312 | tf_op jit(solution)/shard_map/psum | solution.py:34
  567.5 8.2 %copy.11 = f32[3143,768]{1,0:T(8,128)} copy(f32[3143,768]{1,0:T(8,128)} %all-reduce.6.cloned.1.call-done) | data formatting | bytes 19310592
  (5 shorter events, 0.1 us)
Async XLA Ops:
  7.2 441.6 %all-reduce.4.cloned.1.call-start = ((), (), s32[]{:S(2)}) async-start(), calls=%async_computation | async-start | bytes 25165824 | tf_op jit(solution)/shard_map/psum | solution.py:33
  7.2 12.3 %copy-start = (f32[768]{0:T(1024)S(1)}, f32[768]{0:T(1024)}, u32[]{:S(2)}) copy-start(f32[768]{0:T(1024)} %param.9) | copy-start | bytes 9220
  19.5 94.6 %copy-start.1 = (s32[1,4096]{1,0:T(1,128)S(1)}, s32[1,4096]{1,0:T(1,128)}, u32[]{:S(2)}) copy-start(s32[1,4096]{1,0:T(1,128)} %param.7) | copy-start | bytes 49156
  246.7 320.9 %all-reduce.6.cloned.1.call-start = ((), (), s32[]{:S(2)}) async-start(), calls=%async_computation.1 | async-start | bytes 19316736 | tf_op jit(solution)/shard_map/psum | solution.py:34
Sparse Core Ops, SparseCore 0:
  246.8 201.9 all-reduce.3
  451.8 115.7 all-reduce.5
where the time goes:
time: 583 us
  waiting for transfers between devices  253 us (43%)
  blocking collectives  132 us (23%)
  matrix products  88.9 us (15%)
  other arithmetic  85.4 us (15%)
  between operations  14.8 us (3%)
  local copies, waits for them, and re-layouts  8.21 us (1%)
    psum x1, waiting for transfers between devices, local_part(): lax.psum(jnp.einsum('tv,vd->td', dlogits, emb_loc, preferred_element_type...  171 us
    psum x1, waiting for transfers between devices, local_part(): lax.psum(jnp.einsum('tv,td->vd', dlogits, h_act, preferred_element_type=j...  81.5 us
    pmax x1, blocking collectives, local_part(): row_max = lax.pmax(jnp.max(logits, axis=-1, keepdims=True), 'tp')  62.5 us
    psum x1, blocking collectives, local_part(): tok_stats = lax.psum(part_stats, 'tp')  55.9 us
    dot_general x1, matrix products, local_part(): jnp.einsum('td,vd->tv', h_act, emb_loc, preferred_element_type=jnp.float32)  32.1 us
    dot_general x1, matrix products, local_part(): jnp.einsum('tv,td->vd', dlogits, h_act, preferred_element_type=jnp.float32)  29.2 us
    dot_general x1, matrix products, local_part(): jnp.einsum('tv,vd->td', dlogits, emb_loc, preferred_element_type=jnp.floa...  27.6 us
    convert_element_type x1, other arithmetic, local_part(): (jnp.where(is_target, prob_rows - 1.0, prob_rows) * inv_n).astype(jnp.bfl...  26.5 us
  transfers between devices with their start and end apart: 2, of which 2 were waited for; matrix products, arithmetic and copies ran while one was open for 9% of the time, Pallas kernels for 0%

commit v1 on v0

v1 whole, which is shorter than its diff:
```python
import functools

import jax
import jax.numpy as jnp
from jax import lax
from jax.experimental import pallas as pl
from jax.experimental.pallas import tpu as pltpu
from jax.sharding import PartitionSpec as P

NORM_EPS = 1e-5
LANES = 128
MESH = pl.DeviceIdType.MESH
F32 = jnp.float32
BF16 = jnp.bfloat16
VMEM_BYTES = 67_043_328


def _dot(a, b, ca, cb):
    return lax.dot_general(a, b, (((ca,), (cb,)), ((), ())), preferred_element_type=F32)


def _logits_kernel(n_chunk, width, vocab, res_ref, hid_ref, tgt_ref, emb_ref, w_ref, h_ref, e_ref, mc_ref, st_ref):
    rows = res_ref.shape[0]
    resid = res_ref[...] + hid_ref[...].astype(F32)
    inv = lax.rsqrt(jnp.mean(resid * resid, axis=-1, keepdims=True) + NORM_EPS)
    h = (resid * inv * w_ref[...]).astype(BF16)
    h_ref[...] = h
    tgt = tgt_ref[:, 0:1]
    tgt = jnp.where((tgt >= 0) & (tgt < vocab), tgt, -1)
    lane = lax.broadcasted_iota(jnp.int32, (rows, width), 1)
    maxes, sums, picked = [], [], jnp.zeros((rows, 1), F32)
    for c in range(n_chunk):
        cols = pl.ds(c * width, width)
        logits = _dot(h, emb_ref[cols, :], 1, 1)
        if (c + 1) * width > vocab:
            real = lane < vocab - c * width
            peak = jnp.max(jnp.where(real, logits, -jnp.inf), axis=-1, keepdims=True)
            e = jnp.where(real, jnp.exp(logits - peak), 0.0)
        else:
            peak = jnp.max(logits, axis=-1, keepdims=True)
            e = jnp.exp(logits - peak)
        e_ref[:, cols] = e
        picked = picked + jnp.sum(jnp.where(lane == tgt - c * width, logits, 0.0), axis=-1, keepdims=True)
        maxes.append(peak)
        sums.append(jnp.sum(e, axis=-1, keepdims=True))
    top = functools.reduce(jnp.maximum, maxes)
    total = functools.reduce(jnp.add, [s * jnp.exp(m - top) for m, s in zip(maxes, sums)])
    slot = lax.broadcasted_iota(jnp.int32, (rows, LANES), 1)
    marks = jnp.where(slot == n_chunk, tgt.astype(F32), 0.0)
    for c in range(n_chunk):
        marks = jnp.where(slot == c, maxes[c], marks)
    mc_ref[...] = marks
    table = jnp.where(slot == 0, top, jnp.where(slot == 1, total, jnp.where(slot == 2, picked, 0.0)))
    n_tile = rows // LANES
    for j in range(n_tile):
        tile = table[j * LANES:(j + 1) * LANES, :].T
        row = pl.ds(pl.program_id(0) * n_tile + j, 1)
        for k in range(3):
            st_ref[k, row, :] = tile[k:k + 1, :]


def _forward(res, hid, tgt_cols, emb, w, vocab, n_chunk, block):
    n_tok, d = res.shape
    v_pad = emb.shape[0]
    return pl.pallas_call(
        functools.partial(_logits_kernel, n_chunk, v_pad // n_chunk, vocab),
        grid=(n_tok // block,),
        in_specs=[
            pl.BlockSpec((block, d), lambda i: (i, 0)),
            pl.BlockSpec((block, d), lambda i: (i, 0)),
            pl.BlockSpec((block, LANES), lambda i: (i, 0)),
            pl.BlockSpec((v_pad, d), lambda i: (0, 0)),
            pl.BlockSpec((1, d), lambda i: (0, 0)),
        ],
        out_specs=[
            pl.BlockSpec((block, d), lambda i: (i, 0)),
            pl.BlockSpec((block, v_pad), lambda i: (i, 0)),
            pl.BlockSpec((block, LANES), lambda i: (i, 0)),
            pl.BlockSpec((3, n_tok // LANES, LANES), lambda i: (0, 0, 0)),
        ],
        out_shape=[
            jax.ShapeDtypeStruct((n_tok, d), BF16),
            jax.ShapeDtypeStruct((n_tok, v_pad), F32),
            jax.ShapeDtypeStruct((n_tok, LANES), F32),
            jax.ShapeDtypeStruct((3, n_tok // LANES, LANES), F32),
        ],
        compiler_params=pltpu.CompilerParams(dimension_semantics=("arbitrary",), vmem_limit_bytes=60 * 2**20),
    )(res, hid, tgt_cols, emb, w)


def _backward_kernel(n_chunk, inv_n, n_tp,
                     st_ref, w_ref, e_hbm, h_hbm, mc_hbm, emb_hbm, res_hbm, hid_hbm,
                     gr_out, ge_out, small_out,
                     emb, ebuf, mcbuf, hbuf, gbuf, dh, ge, r1, r2, crecv, rx, sy, sz, st2, fin, gro, rown, hown, smb, smr,
                     emb_sem, e_sem, mc_sem, h_sem, own_sem, sy_s, sy_r, sz_s, sz_r, r1_s, r1_r, r2_s, r2_r,
                     ag2_s, ag2_r, ag1_s, ag1_r, out_sem, c_s, c_r, rx_s, rx_r, agx_s, agx_r, agc_s, agc_r, sm_s, sm_r):
    n_tok, d = dh.shape
    v_pad = emb.shape[0]
    width = v_pad // n_chunk
    br = n_tok // 16
    hb = LANES
    n_half = br // hb
    b2 = br // 4
    half_v = v_pad // 2
    bx = v_pad // 16

    tp = lax.axis_index('tp')
    dp = lax.axis_index('dp')
    y, z = lax.rem(tp, 4), lax.div(tp, 4)
    core, x = lax.rem(dp, 2), lax.div(dp, 2)

    def at_tp(dy, dz):
        return {'tp': lax.rem(z + dz, 4) * 4 + lax.rem(y + dy, 4)}

    def at_x(dx):
        return {'dp': lax.rem(x + dx, 4) * 2 + core}

    partner = {'dp': x * 2 + (1 - core)}

    def axis1(c, step):
        return at_tp(step * (1 - c), step * c)

    def axis2(c, step):
        return at_tp(step * c, step * (1 - c))

    def place1(c):
        return y * (1 - c) + z * c

    def place2(c):
        return z * (1 - c) + y * c

    def remote(src, dst, send, recv, device):
        return pltpu.make_async_remote_copy(src_ref=src, dst_ref=dst, send_sem=send, recv_sem=recv,
                                            device_id=device, device_id_type=MESH)

    STEP = (1, 3)

    def rows1(kind, c, s):
        i = place1(c)
        step = 1 + 2 * s
        chunk = lax.rem(i + jnp.where(kind == 0, 2, jnp.where(kind == 3, 0, step)), 4)
        half = jnp.where(kind == 1, 1 - s, s)
        return pl.multiple_of(c * (n_tok // 2) + chunk * (2 * br) + half * br, br)

    def piece_rows(idx):
        k = lax.div(idx, n_half)
        kind, c, s = lax.div(k, 4), lax.rem(lax.div(k, 2), 2), lax.rem(k, 2)
        return pl.multiple_of(rows1(kind, c, s) + lax.rem(idx, n_half) * hb, hb)

    def pieces(idx):
        slot = lax.rem(idx, 2)
        rows = pl.ds(piece_rows(idx), hb)
        return (pltpu.make_async_copy(e_hbm.at[rows, :], ebuf.at[slot], e_sem.at[slot]),
                pltpu.make_async_copy(mc_hbm.at[rows, :], mcbuf.at[slot], mc_sem.at[slot]))

    emb_copy = pltpu.make_async_copy(emb_hbm, emb, emb_sem)
    emb_copy.start()
    for idx in range(2):
        for cp in pieces(idx):
            cp.start()
    own_rows = []
    own_copies = []
    for c in range(2):
        rows = pl.multiple_of(c * (n_tok // 2) + place1(c) * (2 * br) + place2(c) * (2 * b2), 2 * b2)
        own_rows.append(rows)
        own_copies.append(pltpu.make_async_copy(res_hbm.at[pl.ds(rows, 2 * b2), :], rown.at[c], own_sem.at[c, 0]))
        own_copies.append(pltpu.make_async_copy(hid_hbm.at[pl.ds(rows, 2 * b2), :], hown.at[c], own_sem.at[c, 1]))
    for cp in own_copies:
        cp.start()

    barrier = pltpu.get_barrier_semaphore()
    for k in (1, 2, 3):
        for device in (at_tp(k, 0), at_tp(0, k), at_x(k)):
            pl.semaphore_signal(barrier, inc=1, device_id=device, device_id_type=MESH)
    pl.semaphore_signal(barrier, inc=1, device_id=partner, device_id_type=MESH)
    pl.semaphore_wait(barrier, 10)

    def combine(parts):
        top = functools.reduce(jnp.maximum, [p[0] for p in parts])
        total = functools.reduce(jnp.add, [p[1] * jnp.exp(p[0] - top) for p in parts])
        return top, total, functools.reduce(jnp.add, [p[2] for p in parts])

    y_copies = [remote(st_ref, sy.at[k], sy_s.at[k], sy_r.at[k], at_tp(k, 0)) for k in (1, 2, 3)]
    for cp in y_copies:
        cp.start()
    ge[...] = jnp.zeros_like(ge)
    for cp in y_copies:
        cp.wait_recv()
    first = combine([tuple(st_ref[k] for k in range(3))] + [tuple(sy[j, k] for k in range(3)) for j in (1, 2, 3)])
    for k in range(3):
        st2[k] = first[k]
    z_copies = [remote(st2, sz.at[k], sz_s.at[k], sz_r.at[k], at_tp(0, k)) for k in (1, 2, 3)]
    for cp in z_copies:
        cp.start()
    for cp in z_copies:
        cp.wait_recv()
    top, total, picked = combine([first] + [tuple(sz[j, k] for k in range(3)) for j in (1, 2, 3)])
    fin[0] = top
    fin[1] = inv_n / total
    loss = jnp.sum(top + jnp.log(total) - picked) * (inv_n / n_tp)
    emb_copy.wait()

    row_id = lax.broadcasted_iota(jnp.int32, (LANES, LANES), 0)
    lane = lax.broadcasted_iota(jnp.int32, (hb, width), 1)

    def r1_copy(kind, c, s):
        rows = pl.ds(rows1(kind, c, s), br)
        return remote(dh.at[rows, :], r1.at[c, s, kind], r1_s.at[c, s, kind], r1_r.at[c, s, kind], axis1(c, 1 + 2 * s))

    def h_copy(kind, j):
        c, s = lax.div(j, 2), lax.rem(j, 2)
        dst = pl.ds(pl.multiple_of(j * br, br), br)
        return pltpu.make_async_copy(h_hbm.at[pl.ds(rows1(kind, c, s), br), :], hbuf.at[dst, :], h_sem.at[j])

    def block(kind, j):
        c, s = lax.div(j, 2), lax.rem(j, 2)
        h_copy(kind, j).start()
        for hf in range(n_half):
            idx = (kind * 4 + j) * n_half + hf
            slot = lax.rem(idx, 2)
            for cp in pieces(idx):
                cp.wait()
            at = lax.div(piece_rows(idx), LANES)
            cols = jnp.where(row_id == 0, fin[0, pl.ds(at, 1), :], fin[1, pl.ds(at, 1), :]).T
            marks = mcbuf[slot]
            scale = jnp.exp(marks - cols[:, 0:1]) * cols[:, 1:2]
            tgt = marks[:, n_chunk:n_chunk + 1].astype(jnp.int32)
            dst = pl.ds(pl.multiple_of(j * br + hf * hb, hb), hb)
            for v in range(n_chunk):
                g = ebuf[slot, :, v * width:(v + 1) * width] * scale[:, v:v + 1]
                g = g - jnp.where(lane == tgt - v * width, inv_n, 0.0)
                gbuf[dst, v * width:(v + 1) * width] = g.astype(BF16)

            @pl.when(idx + 2 < 16 * n_half)
            def _():
                for cp in pieces(idx + 2):
                    cp.start()
        rows = pl.ds(rows1(kind, c, s), br)
        src = pl.ds(pl.multiple_of(j * br, br), br)
        dh[rows, :] = _dot(gbuf[src, :], emb[...], 1, 0)

        @pl.when(kind < 2)
        def _():
            r1_copy(kind, c, s).start()

        @pl.when(kind == 2)
        def _():
            r1_copy(0, c, s).wait_recv()
            dh[rows, :] = dh[rows, :] + r1[c, s, 0]
            r1_copy(2, c, s).start()

    def group(kind, carry):
        lax.fori_loop(0, 4, lambda j, carry: (block(kind, j), carry)[1], 0)
        for j in range(4):
            h_copy(kind, j).wait()

        def chunk(v, carry):
            cols = pl.ds(pl.multiple_of(v * width, width), width)
            ge[cols, :] = ge[cols, :] + _dot(gbuf[:, cols], hbuf[...], 0, 0)
            return carry

        return lax.fori_loop(0, n_chunk, chunk, carry)

    lax.fori_loop(0, 4, group, 0)

    mine = pl.multiple_of(core * half_v, half_v)
    other = pl.multiple_of((1 - core) * half_v, half_v)
    c_copy = remote(ge.at[pl.ds(other, half_v), :], crecv, c_s, c_r, partner)
    c_copy.start()
    c_copy.wait_recv()

    def add_core(i, carry):
        rows = pl.ds(pl.multiple_of(mine + i * bx, bx), bx)
        ge[rows, :] = ge[rows, :] + crecv[pl.ds(pl.multiple_of(i * bx, bx), bx), :]
        return carry

    lax.fori_loop(0, 8, add_core, 0)

    def rows_x(kind, s):
        chunk = lax.rem(x + (2 if kind == 0 else 0 if kind == 3 else STEP[s]), 4)
        return pl.multiple_of(mine + chunk * (2 * bx) + (1 - s if kind == 1 else s) * bx, bx)

    def rx_copy(kind, s):
        return remote(ge.at[pl.ds(rows_x(kind, s), bx), :], rx.at[s, kind], rx_s.at[s, kind], rx_r.at[s, kind], at_x(STEP[s]))

    for kind in (0, 1):
        for s in range(2):
            rx_copy(kind, s).start()

    for c in range(2):
        for s in range(2):
            r1_copy(1, c, s).wait_recv()
            r1_copy(2, c, s).wait_recv()
    for c in range(2):
        for half in range(2):
            rows = pl.ds(rows1(3, c, half), br)
            dh[rows, :] = dh[rows, :] + r1[c, half, 2] + r1[c, 1 - half, 1]

    def rows2(kind, c, s):
        i = place2(c)
        chunk = lax.rem(i + (2 if kind == 0 else 0 if kind == 3 else STEP[s]), 4)
        half = 1 - s if kind == 1 else s
        return pl.multiple_of(c * (n_tok // 2) + place1(c) * (2 * br) + chunk * (2 * b2) + half * b2, b2)

    def r2_copy(kind, c, s):
        rows = pl.ds(rows2(kind, c, s), b2)
        return remote(dh.at[rows, :], r2.at[c, s, kind], r2_s.at[c, s, kind], r2_r.at[c, s, kind], axis2(c, STEP[s]))

    for kind in (0, 1):
        for c in range(2):
            for s in range(2):
                r2_copy(kind, c, s).start()
    for c in range(2):
        for s in range(2):
            r2_copy(0, c, s).wait_recv()
            rows = pl.ds(rows2(2, c, s), b2)
            dh[rows, :] = dh[rows, :] + r2[c, s, 0]
            r2_copy(2, c, s).start()

    for s in range(2):
        rx_copy(0, s).wait_recv()
        rows = pl.ds(rows_x(2, s), bx)
        ge[rows, :] = ge[rows, :] + rx[s, 0]
        rx_copy(2, s).start()

    for cp in own_copies:
        cp.wait()
    for c in range(2):
        for s in range(2):
            r2_copy(1, c, s).wait_recv()
            r2_copy(2, c, s).wait_recv()
    w = w_ref[...]
    gw = jnp.zeros((1, d), F32)
    ag2_copies, out_copies = [], []
    for c in range(2):
        for half in range(2):
            rows = pl.ds(rows2(3, c, half), b2)
            grad_h = dh[rows, :] + r2[c, half, 2] + r2[c, 1 - half, 1]
            part = pl.ds(half * b2, b2)
            resid = rown[c, part, :] + hown[c, part, :].astype(F32)
            inv = lax.rsqrt(jnp.mean(resid * resid, axis=-1, keepdims=True) + NORM_EPS)
            normed = resid * inv
            dn = grad_h * w
            gro[c, part, :] = inv * (dn - normed * jnp.mean(dn * normed, axis=-1, keepdims=True))
            gw = gw + jnp.sum(grad_h * normed, axis=0, keepdims=True)
        at = pl.ds(own_rows[c], 2 * b2)
        for s in range(2):
            ag2_copies.append(remote(gro.at[c], gr_out.at[at, :], ag2_s.at[c, s, 0], ag2_r.at[c, s, 0], axis2(c, STEP[s])))
            ag2_copies[-1].start()
        out_copies.append(pltpu.make_async_copy(gro.at[c], gr_out.at[at, :], out_sem.at[c]))
        out_copies[-1].start()

    row8 = lax.broadcasted_iota(jnp.int32, (8, d), 0)
    small = jnp.where(row8 == 0, gw, jnp.where(row8 == 1, loss, 0.0))
    small_copies = []

    def small_start(phase, value):
        place = (y, z, x, core)[phase]
        smb[phase] = value
        smr[phase, place] = value
        devices = ([at_tp(k, 0) for k in (1, 2, 3)], [at_tp(0, k) for k in (1, 2, 3)], [at_x(k) for k in (1, 2, 3)], [partner])[phase]
        copies = [remote(smb.at[phase], smr.at[phase, place], sm_s.at[phase, k], sm_r.at[phase, k], device)
                  for k, device in enumerate(devices)]
        for cp in copies:
            cp.start()
        small_copies.extend(copies)
        return copies

    def small_finish(phase, copies):
        for cp in copies:
            cp.wait_recv()
        n = 2 if phase == 3 else 4
        return functools.reduce(jnp.add, [smr[phase, k] for k in range(n)])

    small_step = small_start(0, small)

    def gathered2(c, step):
        return pl.multiple_of(c * (n_tok // 2) + place1(c) * (2 * br) + lax.rem(place2(c) + step, 4) * (2 * b2), 2 * b2)

    fwd2 = []
    for c in range(2):
        for s in range(2):
            ag2_copies[2 * c + s].wait_recv()
            rows = pl.multiple_of(gathered2(c, STEP[1 - s]) + s * b2, b2)
            part = gr_out.at[pl.ds(rows, b2), :]
            fwd2.append(remote(part, part, ag2_s.at[c, s, 1], ag2_r.at[c, s, 1], axis2(c, STEP[s])))
            fwd2[-1].start()
    small_step = small_start(1, small_finish(0, small_step))
    ag1_copies = []
    for c in range(2):
        for s in range(2):
            fwd2[2 * c + s].wait_recv()
        out_copies[c].wait()
        part = gr_out.at[pl.ds(pl.multiple_of(c * (n_tok // 2) + place1(c) * (2 * br), 2 * br), 2 * br), :]
        for s in range(2):
            ag1_copies.append(remote(part, part, ag1_s.at[c, s, 0], ag1_r.at[c, s, 0], axis1(c, STEP[s])))
            ag1_copies[-1].start()
    small_step = small_start(2, small_finish(1, small_step))

    for s in range(2):
        rx_copy(1, s).wait_recv()
        rx_copy(2, s).wait_recv()
    for half in range(2):
        rows = pl.ds(rows_x(3, half), bx)
        ge[rows, :] = ge[rows, :] + rx[half, 2] + rx[1 - half, 1]

    def x_chunk(step):
        return pl.multiple_of(mine + lax.rem(x + step, 4) * (2 * bx), 2 * bx)

    at = pl.ds(x_chunk(0), 2 * bx)
    agx_copies = [remote(ge.at[at, :], ge_out.at[at, :], agx_s.at[s, 0], agx_r.at[s, 0], at_x(STEP[s])) for s in range(2)]
    for cp in agx_copies:
        cp.start()
    agc_copies = [remote(ge.at[at, :], ge_out.at[at, :], agc_s.at[0], agc_r.at[0], partner)]
    agc_copies[-1].start()
    out_copies.append(pltpu.make_async_copy(ge.at[at, :], ge_out.at[at, :], out_sem.at[2]))
    out_copies[-1].start()
    small_step = small_start(3, small_finish(2, small_step))
    small_out[...] = small_finish(3, small_step)

    fwdx = []
    for s in range(2):
        agx_copies[s].wait_recv()
        rows = pl.multiple_of(x_chunk(STEP[1 - s]) + s * bx, bx)
        part = ge_out.at[pl.ds(rows, bx), :]
        fwdx.append(remote(part, part, agx_s.at[s, 1], agx_r.at[s, 1], at_x(STEP[s])))
        fwdx[-1].start()
        whole = ge_out.at[pl.ds(x_chunk(STEP[1 - s]), 2 * bx), :]
        agc_copies.append(remote(whole, whole, agc_s.at[1 + s], agc_r.at[1 + s], partner))
        agc_copies[-1].start()

    fwd1 = []
    for c in range(2):
        for s in range(2):
            ag1_copies[2 * c + s].wait_recv()
            chunk = lax.rem(place1(c) + STEP[1 - s], 4)
            rows = pl.multiple_of(c * (n_tok // 2) + chunk * (2 * br) + s * br, br)
            part = gr_out.at[pl.ds(rows, br), :]
            fwd1.append(remote(part, part, ag1_s.at[c, s, 1], ag1_r.at[c, s, 1], axis1(c, STEP[s])))
            fwd1[-1].start()

    for s in range(2):
        fwdx[s].wait_recv()
        rows = pl.multiple_of(x_chunk(2) + s * bx, bx)
        part = ge_out.at[pl.ds(rows, bx), :]
        agc_copies.append(remote(part, part, agc_s.at[3 + s], agc_r.at[3 + s], partner))
        agc_copies[-1].start()

    for cp in agc_copies + fwd1:
        cp.wait_recv()
    out_copies[2].wait()

    def r1_sent(i, carry):
        r1_copy(lax.div(i, 4), lax.rem(lax.div(i, 2), 2), lax.rem(i, 2)).wait_send()
        return carry

    lax.fori_loop(0, 12, r1_sent, 0)
    for kind in range(3):
        for s in range(2):
            rx_copy(kind, s).wait_send()
            for c in range(2):
                r2_copy(kind, c, s).wait_send()
    for cp in y_copies + z_copies + [c_copy] + ag2_copies + fwd2 + ag1_copies + fwd1 + agx_copies + fwdx + agc_copies + small_copies:
        cp.wait_send()


def _backward(st, w, e, h, mc, emb, res, hid, n_chunk, inv_n, n_tp):
    n_tok, d = res.shape
    v_pad = emb.shape[0]
    br, bx = n_tok // 16, v_pad // 16
    b2 = br // 4
    tiles = n_tok // LANES
    dma = pltpu.SemaphoreType.DMA
    any_spec = pl.BlockSpec(memory_space=pl.ANY)
    vmem_spec = pl.BlockSpec(memory_space=pltpu.VMEM)
    flops = 4 * n_tok * v_pad * d
    return pl.pallas_call(
        functools.partial(_backward_kernel, n_chunk, inv_n, n_tp),
        in_specs=[vmem_spec, vmem_spec] + [any_spec] * 6,
        out_specs=[any_spec, any_spec, vmem_spec],
        out_shape=[
            jax.ShapeDtypeStruct((n_tok, d), F32),
            jax.ShapeDtypeStruct((v_pad, d), F32),
            jax.ShapeDtypeStruct((8, d), F32),
        ],
        scratch_shapes=[
            pltpu.VMEM((v_pad, d), BF16),
            pltpu.VMEM((2, LANES, v_pad), F32),
            pltpu.VMEM((2, LANES, LANES), F32),
            pltpu.VMEM((4 * br, d), BF16),
            pltpu.VMEM((4 * br, v_pad), BF16),
            pltpu.VMEM((n_tok, d), F32),
            pltpu.VMEM((v_pad, d), F32),
            pltpu.VMEM((2, 2, 3, br, d), F32),
            pltpu.VMEM((2, 2, 3, b2, d), F32),
            pltpu.VMEM((v_pad // 2, d), F32),
            pltpu.VMEM((2, 3, bx, d), F32),
            pltpu.VMEM((4, 3, tiles, LANES), F32),
            pltpu.VMEM((4, 3, tiles, LANES), F32),
            pltpu.VMEM((3, tiles, LANES), F32),
            pltpu.VMEM((2, tiles, LANES), F32),
            pltpu.VMEM((2, 2 * b2, d), F32),
            pltpu.VMEM((2, 2 * b2, d), F32),
            pltpu.VMEM((2, 2 * b2, d), BF16),
            pltpu.VMEM((4, 8, d), F32),
            pltpu.VMEM((4, 4, 8, d), F32),
            dma, dma((2,)), dma((2,)), dma((4,)), dma((2, 2)),
            dma((4,)), dma((4,)), dma((4,)), dma((4,)),
            dma((2, 2, 3)), dma((2, 2, 3)), dma((2, 2, 3)), dma((2, 2, 3)),
            dma((2, 2, 2)), dma((2, 2, 2)), dma((2, 2, 2)), dma((2, 2, 2)),
            dma((3,)), dma, dma, dma((2, 3)), dma((2, 3)), dma((2, 2)), dma((2, 2)),
            dma((5,)), dma((5,)), dma((4, 3)), dma((4, 3)),
        ],
        compiler_params=pltpu.CompilerParams(collective_id=0, has_side_effects=True, vmem_limit_bytes=VMEM_BYTES),
        cost_estimate=pl.CostEstimate(flops=flops, bytes_accessed=4 * n_tok * v_pad, transcendentals=0),
    )(st, w, e, h, mc, emb, res, hid)


def solution(mesh, n_chunk=5, width=640, block=512):
    def program(hidden, residual, targets, embedding, norm_w):
        inv_n = 1.0 / (hidden.shape[0] * hidden.shape[1])
        n_tp = mesh.shape['tp']

        def local_part(hid_loc, res_loc, tgt_loc, emb_loc, norm_vec):
            n_batch, n_seq, d = hid_loc.shape
            n_tok = n_batch * n_seq
            vocab = emb_loc.shape[0]
            v_pad = n_chunk * width
            hid, res = hid_loc.reshape(n_tok, d), res_loc.reshape(n_tok, d)
            ids = tgt_loc.reshape(n_tok) - lax.axis_index('tp') * vocab
            tgt_cols = jnp.broadcast_to(ids[:, None], (n_tok, LANES))
            emb = jnp.pad(emb_loc, ((0, v_pad - vocab), (0, 0)))
            w = norm_vec.reshape(1, d)
            h, e, mc, st = _forward(res, hid, tgt_cols, emb, w, vocab, n_chunk, block)
            gr, ge, small = _backward(st, w, e, h, mc, emb, res, hid, n_chunk, inv_n, n_tp)
            return small[1, 0], gr.reshape(n_batch, n_seq, d), ge[:vocab], small[0]

        sharded = jax.shard_map(
            local_part, mesh=mesh,
            in_specs=(P('dp', None, None), P('dp', None, None), P('dp', None), P('tp', None), P(None)),
            out_specs=(P(), P('dp', None, None), P('tp', None), P(None)),
            check_vma=False)
        return sharded(hidden, residual, targets, embedding, norm_w)

    return program
```

time: 583 us -> 259 us (0.44)
  waiting for transfers between devices: 253 us -> 0 us
  Pallas kernels: 0 us -> 227 us
  blocking collectives: 132 us -> 0 us
  matrix products: 88.9 us -> 0 us
  other arithmetic: 85.4 us -> 0.73 us
  local copies, waits for them, and re-layouts: 8.21 us -> 30 us
  between operations: 14.8 us -> 0.65 us
    psum x2 -> x0, waiting for transfers between devices: 253 us -> none  [the longest x1 171 us: local_part(): lax.psum(jnp.einsum('tv,vd->td', dlogits, emb_loc, preferred_element_type...]
    pallas_call x0 -> x2, Pallas kernels: none -> 227 us  [the longest x1 187 us: _backward(): pl.pallas_call(functools.partial(_backward_kernel, n_chunk, inv_n, n_tp),...]
    dot_general x3 -> x0, matrix products: 88.9 us -> none  [the longest x1 32.1 us: local_part(): jnp.einsum('td,vd->tv', h_act, emb_loc, preferred_element_type=jnp.float32)]
    psum x2 -> x0, blocking collectives: 69.6 us -> none  [the longest x1 55.9 us: local_part(): tok_stats = lax.psum(part_stats, 'tp')]
    pmax x1 -> x0, blocking collectives: 62.5 us -> none  [local_part(): row_max = lax.pmax(jnp.max(logits, axis=-1, keepdims=True), 'tp')]
    reduce_sum x4 -> x0, other arithmetic: 44.7 us -> none  [the longest x1 22.5 us: local_part(): jnp.sum(exp_shift, axis=-1)]
    convert_element_type x1 -> x0, other arithmetic: 26.5 us -> none  [local_part(): (jnp.where(is_target, prob_rows - 1.0, prob_rows) * inv_n).astype(jnp.bfl...]
    reshape x1 -> x0, other arithmetic: 14.2 us -> none  [local_part(): grad_r.reshape(n_batch, n_seq, d_model)]
  transfers between devices with their start and end apart: 2 -> 0, of which waited for: 2 -> 0; matrix products, arithmetic and copies ran while one was open for 9% -> 0% of each run, Pallas kernels for 0% -> 0%
where the time goes in v1:
time: 259 us
  Pallas kernels  227 us (88%)
  local copies, waits for them, and re-layouts  30 us (12%)
    pallas_call x1, Pallas kernels, _backward(): pl.pallas_call(functools.partial(_backward_kernel, n_chunk, inv_n, n_tp),...  187 us
    pallas_call x1, Pallas kernels, _forward(): pl.pallas_call(functools.partial(_logits_kernel, n_chunk, v_pad // n_chun...  39.8 us
    slice x3, local copies, waits for them, and re-layouts, local_part(): return (small[1, 0], gr.reshape(n_batch, n_seq, d), ge[:vocab], small[0])  10.7 us
    unnamed x1, local copies, waits for them, and re-layouts  10.2 us

profile of v1, /device:TPU:1, one launch (start us, length us, event | category | flops | bytes accessed | tf_op | source)
XLA Modules:
  0.0 258.6 jit_solution(2439612739270561824)
XLA Ops:
  0.6 1.3 reshape.30.w_ref
  1.9 0.7 broadcast_subtract_fusion
  2.6 3.0 %broadcast_in_dim.2.tgt_ref = s32[4096,128]{1,0:T(8,128)} broadcast(s32[4096]{0:T(1024)S(1)} %bitcast.10), dimensions={0} | broadcast | bytes 2113536 | tf_op jit(solution)/shard_map/broadcast_in_dim | solution.py:531
  5.6 4.9 %pad.4.emb_ref.emb_hbm = bf16[3200,768]{1,0:T(8,128)(2,1)} pad(bf16[3143,768]{1,0:T(8,128)(2,1)} %param.8, bf16[]{:T(256)} %constant.10.clone.1), padding=0_57x0_0 | pad | bytes 9742850 | tf_op jit(solution)/shard_map/jit(_pad)/pad | solution.py:532
  10.5 39.8 %shard_map.84 = (bf16[4096,768]{1,0:T(8,128)(2,1)}, f32[4096,3200]{1,0:T(8,128)}, f32[4096,128]{1,0:T(8,128)}, f32[3,32,128]{2,1,0:T(8,128)}) custom-call(f32[4096,768]{1,0:T(8,128)} %bitcast.6, bf16[4096,768]{1,0:T(8,128)(2,1)} %bitcast.8, s32[4096,128]{1,0:T(8,128)} %broadcast_in_dim.2.tgt_ref, bf16[3200,768]{1,0:T(8,128)(2,1)} %pad.4.emb_ref.emb_hbm, ...), custom_call_target="tpu_custom_call" | custom-call | tf_op jit(solution)/shard_map/pallas_call | solution.py:65
  50.3 187.4 %shard_map.85 = (f32[4096,768]{1,0:T(8,128)}, f32[3200,768]{1,0:T(8,128)}, f32[8,768]{1,0:T(8,128)}) custom-call(f32[3,32,128]{2,1,0:T(8,128)} %get-tuple-element.11.st_ref, f32[1,768]{1,0:T(1,128)} %reshape.30.w_ref, f32[4096,3200]{1,0:T(8,128)} %get-tuple-element.12.e_hbm, bf16[4096,768]{1,0:T(8,128)(2,1)} %get-tuple-element.13.h_hbm, ...), custom_call_target="tpu_custom_call" | custom-call | flops 40265318400 | bytes 52428800 | tf_op jit(solution)/shard_map/pallas_call | solution.py:477
  237.8 1.2 slice.9
  238.9 1.3 slice_reduce_fusion
  240.3 8.2 %slice.10 = f32[3143,768]{1,0:T(8,128)} slice(f32[3200,768]{1,0:T(8,128)} %get-tuple-element.17), slice={[0:3143], [0:768]} | slice | bytes 19310592 | tf_op jit(solution)/shard_map/slice | solution.py:536
  248.5 10.2 %copy.10 = f32[1,4096,768]{2,1,0:T(8,128)} copy(f32[1,4096,768]{2,1,0:T(8,128)} %bitcast.5) | data formatting | bytes 25165824

commit v2 on v0

v2 whole, which is shorter than its diff:
```python
import functools

import jax
import jax.numpy as jnp
from jax import lax
from jax.experimental import pallas as pl
from jax.experimental.pallas import tpu as pltpu
from jax.sharding import PartitionSpec as P

NORM_EPS = 1e-5
LANES = 128
MESH = pl.DeviceIdType.MESH
ROWS = 16
WIDE = 512
PAIR = (0, 1)
OTHERS = (1, 2, 3)
TWO = 2
RING = 4
F32 = jnp.float32
BF16 = jnp.bfloat16
VMEM_BYTES = 67_043_328
STEP = (1, 3)


class _Copy:
    def __init__(self, make, *args):
        self.make = functools.partial(make, *args)

    def start(self):
        self.make().start()

    def wait_recv(self):
        self.make().wait_recv()

    def wait_send(self):
        self.make().wait_send()


def _dot(a, b, ca, cb):
    return lax.dot_general(a, b, (((ca,), (cb,)), ((), ())), preferred_element_type=F32)


def _kernel(chunks, vocab, inv_n, n_tp,
            tgt_ref, w_ref, tail_ref, emb_hbm, res_hbm, hid_hbm,
            gr_out, ge_out, small_out, h_hbm, e_hbm, mc_hbm, g_hbm,
            emb, dh, ge, r1, r2, crecv, rx, st, sy, sz, st2, fin, rown, hown, losses, smb, smr,
            emb_sem, in_sem, l_sem, e_sem, gw_sem, gin_sem, hin_sem, own_sem, sy_s, sy_r, sz_s, sz_r, r1_s, r1_r, r2_s, r2_r,
            ag2_s, ag2_r, ag1_s, ag1_r, out_sem, c_s, c_r, rx_s, rx_r, agx_s, agx_r, agc_s, agc_r, sm_s, sm_r):
    n_tok, d = dh.shape
    v_pad = emb.shape[0]
    mw = (len(chunks) + 1) * LANES
    rb = 2 * LANES
    n_blk = n_tok // rb
    br = n_tok // 32
    b2 = br // 4
    dx = d // 2
    cx = v_pad // 4
    bx = cx // 2
    wx = ge.shape[1]
    ox = (cx // LANES) * LANES
    sl_rows = n_tok // 2

    tp = lax.axis_index('tp')
    dp = lax.axis_index('dp')
    y, z = lax.rem(tp, 4), lax.div(tp, 4)
    core, x = lax.rem(dp, 2), lax.div(dp, 2)

    def at_tp(dy, dz):
        return {'tp': lax.rem(z + dz, 4) * 4 + lax.rem(y + dy, 4)}

    def at_x(k):
        return {'dp': lax.rem(x + k, 4) * 2 + core}

    partner = {'dp': x * 2 + (1 - core)}

    def axis1(c, step):
        return at_tp(step * (1 - c), step * c)

    def axis2(c, step):
        return at_tp(step * c, step * (1 - c))

    def place1(c):
        return y * (1 - c) + z * c

    def place2(c):
        return z * (1 - c) + y * c

    def remote(src, dst, send, recv, device):
        return pltpu.make_async_remote_copy(src_ref=src, dst_ref=dst, send_sem=send, recv_sem=recv,
                                            device_id=device, device_id_type=MESH)

    def start(copies):
        for cp in copies:
            cp.start()

    def wait(copies):
        for cp in copies:
            cp.wait()

    sent = []

    def send(copies):
        start(copies)
        sent.extend(copies)
        return copies

    def recv(copies):
        for cp in copies:
            cp.wait_recv()

    barrier = pltpu.get_barrier_semaphore()
    for k in OTHERS:
        for device in (at_tp(k, 0), at_tp(0, k), at_x(k)):
            pl.semaphore_signal(barrier, inc=1, device_id=device, device_id_type=MESH)
    pl.semaphore_signal(barrier, inc=1, device_id=partner, device_id_type=MESH)

    whole = (vocab // 16) * 16
    tail = jnp.where(lax.broadcasted_iota(jnp.int32, (16, d), 0) < vocab - whole, tail_ref[...].astype(F32), 0.0)
    emb[whole:whole + 16, :] = tail.astype(BF16)
    emb[whole + 16:, :] = jnp.zeros((v_pad - whole - 16, d), BF16)
    emb_copy = pltpu.make_async_copy(emb_hbm.at[pl.ds(0, whole), :], emb.at[pl.ds(0, whole), :], emb_sem)
    emb_copy.start()
    own_rows, own_copies = [], []
    for sl in PAIR:
        for c in PAIR:
            rows = pl.multiple_of(sl * sl_rows + c * (sl_rows // 2) + place1(c) * (2 * br) + place2(c) * (2 * b2), 2 * b2)
            own_rows.append(rows)
            own_copies.append(pltpu.make_async_copy(res_hbm.at[pl.ds(rows, 2 * b2), :], rown.at[sl, c], own_sem.at[sl, c, 0]))
            own_copies.append(pltpu.make_async_copy(hid_hbm.at[pl.ds(rows, 2 * b2), :], hown.at[sl, c], own_sem.at[sl, c, 1]))

    def combine(parts):
        top = functools.reduce(jnp.maximum, [p[0] for p in parts])
        total = functools.reduce(jnp.add, [p[1] * jnp.exp(p[0] - top) for p in parts])
        return top, total, functools.reduce(jnp.add, [p[2] for p in parts])

    def stats_y(sl):
        return send([_Copy(lambda k: remote(st.at[sl], sy.at[sl, k], sy_s.at[sl, k], sy_r.at[sl, k], at_tp(k, 0)), k) for k in OTHERS])

    def stats_z(sl, copies):
        recv(copies)
        parts = combine([tuple(st[sl, k] for k in range(3))] + [tuple(sy[sl, j, k] for k in range(3)) for j in OTHERS])
        for k in range(3):
            st2[sl, k] = parts[k]
        return send([_Copy(lambda k: remote(st2.at[sl], sz.at[sl, k], sz_s.at[sl, k], sz_r.at[sl, k], at_tp(0, k)), k) for k in OTHERS])

    tiles_sl = sl_rows // LANES

    def stats_end(sl, copies):
        recv(copies)
        top, total, picked = combine([tuple(st2[sl, k] for k in range(3))] + [tuple(sz[sl, j, k] for k in range(3)) for j in OTHERS])
        fin[0, sl * tiles_sl:(sl + 1) * tiles_sl, :] = top
        fin[1, sl * tiles_sl:(sl + 1) * tiles_sl, :] = inv_n / total
        part = (top + jnp.log(total) - picked) * (inv_n / n_tp)
        losses[sl] = jnp.sum(jnp.sum(part, axis=0, keepdims=True), axis=1, keepdims=True) + jnp.zeros((8, LANES), F32)

    ahead = {}

    def block_rows(i):
        return pl.ds(pl.multiple_of(i * rb, rb), rb)

    def logits_stage(ebuf, mcbuf, rbuf, hbuf, hobuf, sums, picks, ids):
        def kept(v, first, size, k, width):
            return v, pl.ds((k // d) * rb + first, size), pl.ds(k % d, width)

        def loads(i):
            slot, rows = lax.rem(i, 2), block_rows(i)
            return (pltpu.make_async_copy(res_hbm.at[rows, :], rbuf.at[slot], in_sem.at[slot, 0, 0]),
                    pltpu.make_async_copy(hid_hbm.at[rows, :], hbuf.at[slot], in_sem.at[slot, 0, 1]))

        def stores(i):
            slot, rows = lax.rem(i, 2), block_rows(i)
            return (pltpu.make_async_copy(hobuf.at[slot], h_hbm.at[rows, :], l_sem.at[slot, 0, 0]),
                    pltpu.make_async_copy(ebuf.at[slot], e_hbm.at[rows, :], l_sem.at[slot, 0, 1]),
                    pltpu.make_async_copy(mcbuf.at[slot], mc_hbm.at[rows, :], l_sem.at[slot, 1, 0]))

        step = {}

        def one(i, carry):
            slot = lax.rem(i, 2)

            @pl.when(i == n_blk // 2)
            def _():
                pl.semaphore_wait(barrier, 10)
                step['y'] = stats_y(0)
                start(own_copies)

            @pl.when(i == 3 * n_blk // 4)
            def _():
                step['z'] = stats_z(0, step['y'])

            wait(loads(i))

            @pl.when(i >= 2)
            def _():
                wait(stores(i - 2))

            resid = rbuf[slot] + hbuf[slot].astype(F32)
            inv = lax.rsqrt(jnp.mean(resid * resid, axis=-1, keepdims=True) + NORM_EPS)
            h = (resid * inv * w_ref[...]).astype(BF16)
            hobuf[slot] = h
            for j in range(rb // LANES):
                row = (tgt_ref[pl.ds(i * (rb // LANES) + j, 1), :] - tp * vocab).astype(F32)
                col = jnp.broadcast_to(row, (LANES, LANES)).T
                ids[j * LANES:(j + 1) * LANES, :] = jnp.where((col >= 0) & (col < vocab), col, -1.0)
            mcbuf[slot, :, len(chunks) * LANES:] = ids[...]

            def finish(v):
                at = sum(chunks[:v])

                def some(r, carry):
                    first = pl.multiple_of(r * ROWS, ROWS)
                    rows = pl.ds(first, ROWS)
                    tgt = ids[rows, :].astype(jnp.int32)
                    tiles = [ge[kept(v, first, ROWS, k, LANES)] for k in range(0, chunks[v], LANES)]
                    pick = jnp.zeros((ROWS, LANES), F32)
                    for k, tile in enumerate(tiles):
                        pick = pick + jnp.where(lane == tgt - (at + k * LANES), tile, 0.0)
                    real = lane < vocab - (at + chunks[v] - LANES)
                    if at + chunks[v] > vocab:
                        top = functools.reduce(jnp.maximum, tiles[:-1] + [jnp.where(real, tiles[-1], -jnp.inf)])
                    else:
                        top = functools.reduce(jnp.maximum, tiles)
                    total = jnp.zeros((ROWS, LANES), F32)
                    for k, tile in enumerate(tiles):
                        e = jnp.exp(tile - top)
                        if at + (k + 1) * LANES > vocab:
                            e = jnp.where(real, e, 0.0)
                        ebuf[slot, rows, at + k * LANES:at + (k + 1) * LANES] = e
                        total = total + e
                    mcbuf[slot, rows, v * LANES:(v + 1) * LANES] = top
                    sums[v, rows, :] = total
                    picks[v, rows, :] = pick
                    return carry

                lax.fori_loop(0, rb // ROWS, some, 0, unroll=True)

            lane = lax.broadcasted_iota(jnp.int32, (ROWS, LANES), 1)
            at = 0
            for v, width in enumerate(chunks):
                for k in range(0, width, d):
                    part = min(d, width - k)
                    ge[kept(v, 0, rb, k, part)] = _dot(h, emb[at + k:at + k + part, :], 1, 1)
                if v:
                    finish(v - 1)
                at += width
            finish(len(chunks) - 1)
            maxes = [mcbuf[slot, :, v * LANES:(v + 1) * LANES] for v in range(len(chunks))]
            top = jnp.max(functools.reduce(jnp.maximum, maxes), axis=-1, keepdims=True)
            total = functools.reduce(jnp.add, [sums[v] * jnp.exp(m - top) for v, m in enumerate(maxes)])
            total = jnp.sum(total, axis=-1, keepdims=True)
            picked = jnp.sum(functools.reduce(jnp.add, [picks[v] for v in range(len(chunks))]), axis=-1, keepdims=True)
            lane = lax.broadcasted_iota(jnp.int32, (rb, LANES), 1)
            table = jnp.where(lane == 0, top, jnp.where(lane == 1, total, picked))
            sl = lax.div(i, n_blk // 2)
            for j in range(rb // LANES):
                tile = table[j * LANES:(j + 1) * LANES, :].T
                row = pl.ds((i - sl * (n_blk // 2)) * (rb // LANES) + j, 1)
                for k in range(3):
                    st[sl, k, row, :] = tile[k:k + 1, :]
            start(stores(i))

            @pl.when(i + 2 < n_blk)
            def _():
                start(loads(i + 2))

            return carry

        start(loads(0))
        start(loads(1))
        emb_copy.wait()
        lax.fori_loop(0, n_blk, one, 0)
        ahead['y'] = stats_y(1)
        wait(stores(n_blk - 2))
        wait(stores(n_blk - 1))
        stats_end(0, step['z'])

    def rows1(sl, kind, c, s):
        step = 1 + 2 * s
        chunk = lax.rem(place1(c) + jnp.where(kind == 0, 2, jnp.where(kind == 3, 0, step)), 4)
        half = jnp.where(kind == 1, 1 - s, s)
        return pl.multiple_of(sl * sl_rows + c * (sl_rows // 2) + chunk * (2 * br) + half * br, br)

    def r1_copy(sl, kind, c, s):
        rows = pl.ds(rows1(sl, kind, c, s), br)
        return remote(dh.at[rows, :], r1.at[sl, c, s, kind], r1_s.at[sl, c, s, kind], r1_r.at[sl, c, s, kind], axis1(c, 1 + 2 * s))

    def gradient_stage(ebuf, mcbuf, gbuf0, gbuf1, spread):
        gbufs = (gbuf0, gbuf1)
        row_id = lax.broadcasted_iota(jnp.int32, (LANES, LANES), 0)
        lane = lax.broadcasted_iota(jnp.int32, (ROWS, WIDE), 1)

        def piece(b, c, s):
            b = lax.rem(b, n_blk)
            return rows1(lax.div(b, 8), lax.rem(lax.div(b, 2), 4), c, s)

        def loads(b, c):
            out = []
            for s in PAIR:
                rows = pl.ds(piece(b, c, s), br)
                part = pl.ds(s * br, br)
                out.append(pltpu.make_async_copy(e_hbm.at[rows, :], ebuf.at[c, part, :], e_sem.at[c, s, 0]))
                out.append(pltpu.make_async_copy(mc_hbm.at[rows, :], mcbuf.at[c, part, :], e_sem.at[c, s, 1]))
            return out

        def stores(b, c):
            return [pltpu.make_async_copy(gbufs[c].at[pl.ds(s * br, br), :], g_hbm.at[pl.ds(piece(b, c, s), br), :], gw_sem.at[c, s, 0])
                    for s in PAIR]

        def prepare(b, c):
            for s in PAIR:
                at = lax.div(piece(b, c, s), LANES)
                cols = jnp.where(row_id == 0, fin[0, pl.ds(at, 1), :], fin[1, pl.ds(at, 1), :]).T
                part = slice(s * br, (s + 1) * br)
                for v in range(len(chunks)):
                    lanes = slice(v * LANES, (v + 1) * LANES)
                    spread[v, part, :] = jnp.exp(mcbuf[c, part, lanes] - cols[:, 0:1]) * cols[:, 1:2]

        def make_g(c, unroll=True):
            def some(r, carry):
                rows = pl.ds(pl.multiple_of(r * ROWS, ROWS), ROWS)
                tgt = mcbuf[c, rows, len(chunks) * LANES:].astype(jnp.int32)
                at = 0
                for v, width in enumerate(chunks):
                    scale = spread[v, rows, :]
                    for k in range(at, at + width, WIDE):
                        n = min(WIDE, at + width - k)
                        hit = lane[:, :n] == jnp.concatenate([tgt - k] * (n // LANES), axis=1)
                        g = ebuf[c, rows, k:k + n] * jnp.concatenate([scale] * (n // LANES), axis=1) - jnp.where(hit, inv_n, 0.0)
                        gbufs[c][rows, k:k + n] = g.astype(BF16)
                    at += width
                return carry

            lax.fori_loop(0, rb // ROWS, some, 0, unroll=unroll)

        def step(b, c):
            nb, nc = b + 1, 1 - c
            sl, kind = lax.div(b, 8), lax.rem(lax.div(b, 2), 4)
            wait(loads(nb, nc))

            @pl.when(nb >= 2)
            def _():
                wait(stores(nb - 2, nc))

            prepare(nb, nc)
            rows = [pl.ds(rows1(sl, kind, c, s), br) for s in PAIR]

            make_g(nc)
            value = _dot(gbufs[c][...], emb[...], 1, 0)
            for s in PAIR:
                dh[rows[s], :] = value[s * br:(s + 1) * br, :]

            @pl.when(nb < n_blk)
            def _():
                start(stores(nb, nc))

            @pl.when(nb + 2 <= n_blk)
            def _():
                start(loads(nb + 2, nc))

            @pl.when(kind < 2)
            def _():
                for s in PAIR:
                    r1_copy(sl, kind, c, s).start()

            @pl.when(kind == 2)
            def _():
                for s in PAIR:
                    r1_copy(sl, 0, c, s).wait_recv()
                    rows = pl.ds(rows1(sl, kind, c, s), br)
                    dh[rows, :] = dh[rows, :] + r1[sl, c, s, 0]
                    r1_copy(sl, 2, c, s).start()

        def pair(kk, carry):
            @pl.when(kk == 2)
            def _():
                stats_end(1, ahead['z'])

            step(2 * kk, 0)
            step(2 * kk + 1, 1)
            return carry

        start(loads(0, 0))
        start(loads(1, 1))
        wait(loads(0, 0))
        prepare(0, 0)
        make_g(0, False)
        start(stores(0, 0))
        start(loads(2, 0))
        ahead['z'] = stats_z(1, ahead['y'])
        lax.fori_loop(0, n_blk // 2, pair, 0)
        wait(stores(n_blk - 1, 1))

    def rows2(sl, kind, c, s):
        chunk = lax.rem(place2(c) + (2 if kind == 0 else 0 if kind == 3 else STEP[s]), 4)
        half = 1 - s if kind == 1 else s
        return pl.multiple_of(sl * sl_rows + c * (sl_rows // 2) + place1(c) * (2 * br) + chunk * (2 * b2) + half * b2, b2)

    def r2_copy(sl, kind, c, s):
        rows = pl.ds(rows2(sl, kind, c, s), b2)
        return remote(dh.at[rows, :], r2.at[sl, c, s, kind], r2_s.at[sl, c, s, kind], r2_r.at[sl, c, s, kind], axis2(c, STEP[s]))

    def first_end(sl):
        for c in PAIR:
            for s in PAIR:
                r1_copy(sl, 1, c, s).wait_recv()
                r1_copy(sl, 2, c, s).wait_recv()
        for c in PAIR:
            for half in PAIR:
                rows = pl.ds(rows1(sl, 3, c, half), br)
                dh[rows, :] = dh[rows, :] + r1[sl, c, half, 2] + r1[sl, c, 1 - half, 1]
        send([_Copy(r2_copy, sl, kind, c, s) for kind in (0, 1) for c in PAIR for s in PAIR])

    def second_relay(sl):
        for c in PAIR:
            for s in PAIR:
                r2_copy(sl, 0, c, s).wait_recv()
                rows = pl.ds(rows2(sl, 2, c, s), b2)
                dh[rows, :] = dh[rows, :] + r2[sl, c, s, 0]
                send([_Copy(r2_copy, sl, 2, c, s)])

    out_copies = []

    def ag2_copy(sl, c, s):
        at = pl.ds(own_rows[2 * sl + c], 2 * b2)
        return remote(dh.at[at, :], gr_out.at[at, :], ag2_s.at[sl, c, s, 0], ag2_r.at[sl, c, s, 0], axis2(c, STEP[s]))

    def own_copy(sl, c):
        at = pl.ds(own_rows[2 * sl + c], 2 * b2)
        return pltpu.make_async_copy(dh.at[at, :], gr_out.at[at, :], out_sem.at[2 * sl + c])

    def second_end(sl):
        for c in PAIR:
            for s in PAIR:
                r2_copy(sl, 1, c, s).wait_recv()
                r2_copy(sl, 2, c, s).wait_recv()
        w = w_ref[...]
        gw = jnp.zeros((1, d), F32)
        copies = []
        for c in PAIR:
            for half in PAIR:
                rows = pl.ds(rows2(sl, 3, c, half), b2)
                grad_h = dh[rows, :] + r2[sl, c, half, 2] + r2[sl, c, 1 - half, 1]
                part = pl.ds(half * b2, b2)
                resid = rown[sl, c, part, :] + hown[sl, c, part, :].astype(F32)
                inv = lax.rsqrt(jnp.mean(resid * resid, axis=-1, keepdims=True) + NORM_EPS)
                normed = resid * inv
                dn = grad_h * w
                dh[rows, :] = inv * (dn - normed * jnp.mean(dn * normed, axis=-1, keepdims=True))
                gw = gw + jnp.sum(grad_h * normed, axis=0, keepdims=True)
            copies += send([_Copy(ag2_copy, sl, c, s) for s in PAIR])
            out_copies.append(_Copy(own_copy, sl, c))
            out_copies[-1].start()
        return gw, copies

    def own_chunk(sl, c, k):
        return pl.multiple_of(sl * sl_rows + c * (sl_rows // 2) + lax.rem(place1(c) + k, 4) * (2 * br), 2 * br)

    def fwd2_copy(sl, c, s):
        rows = pl.multiple_of(own_chunk(sl, c, 0) + lax.rem(place2(c) + STEP[1 - s], 4) * (2 * b2) + s * b2, b2)
        part = gr_out.at[pl.ds(rows, b2), :]
        return remote(part, part, ag2_s.at[sl, c, s, 1], ag2_r.at[sl, c, s, 1], axis2(c, STEP[s]))

    def gather2(sl, copies):
        out = []
        for c in PAIR:
            for s in PAIR:
                copies[2 * c + s].wait_recv()
                out += send([_Copy(fwd2_copy, sl, c, s)])
        return out

    def ag1_copy(sl, c, s):
        part = gr_out.at[pl.ds(own_chunk(sl, c, 0), 2 * br), :]
        return remote(part, part, ag1_s.at[sl, c, s, 0], ag1_r.at[sl, c, s, 0], axis1(c, STEP[s]))

    def gather1_start(sl, copies):
        out = []
        for c in PAIR:
            recv(copies[2 * c:2 * c + 2])
            out_copies[2 * sl + c].make().wait()
            out += send([_Copy(ag1_copy, sl, c, s) for s in PAIR])
        return out

    def fwd1_copy(sl, c, s):
        part = gr_out.at[pl.ds(pl.multiple_of(own_chunk(sl, c, STEP[1 - s]) + s * br, br), br), :]
        return remote(part, part, ag1_s.at[sl, c, s, 1], ag1_r.at[sl, c, s, 1], axis1(c, STEP[s]))

    def gather1(sl, copies):
        out = []
        for c in PAIR:
            for s in PAIR:
                copies[2 * c + s].wait_recv()
                out += send([_Copy(fwd1_copy, sl, c, s)])
        return out

    order = (2, 1, 3, 0)
    mine = pl.ds(pl.multiple_of(core * dx, LANES), dx)
    other = pl.ds(pl.multiple_of((1 - core) * dx, LANES), dx)

    def x_index(j):
        return lax.rem(x + order[j], 4)

    def x_base(j):
        return x_index(j) * (cx - ox)

    def c_copy(j):
        rows = pl.ds(pl.multiple_of(x_base(j), 8), cx)
        return remote(ge.at[j, rows, other], crecv.at[j], c_s.at[j], c_r.at[j], partner)

    def core_end(j):
        c_copy(j).wait_recv()

        def add(i, carry):
            rows = pl.ds(pl.multiple_of(x_base(j) + i * (cx // 4), 8), cx // 4)
            ge[j, rows, mine] = ge[j, rows, mine] + crecv[j, pl.ds(pl.multiple_of(i * (cx // 4), 8), cx // 4), :]
            return carry

        lax.fori_loop(0, 4, add, 0)

    def rows_x(kind, s):
        j = 0 if kind == 0 else 3 if kind == 3 else 1 + s
        half = 1 - s if kind == 1 else s
        return j, pl.ds(pl.multiple_of(x_base(j) + half * bx, 8), bx)

    def rx_copy(kind, s):
        j, rows = rows_x(kind, s)
        return remote(ge.at[j, rows, mine], rx.at[s, kind], rx_s.at[s, kind], rx_r.at[s, kind], at_x(STEP[s]))

    def embed_stage(gbuf, hbuf):
        kb = n_tok // 4

        def loads(t):
            slot, rows = lax.rem(t, 2), pl.ds(pl.multiple_of(lax.rem(t, 4) * kb, kb), kb)
            first = lax.rem(x + jnp.where(t < 4, 2, jnp.where(t < 8, 1, jnp.where(t < 12, 3, 0))), 4)
            cols = pl.ds(pl.multiple_of(first * ox, LANES), wx)
            return (pltpu.make_async_copy(g_hbm.at[rows, cols], gbuf.at[slot], gin_sem.at[slot]),
                    pltpu.make_async_copy(h_hbm.at[rows, :], hbuf.at[slot], hin_sem.at[slot]))

        def chunk(j):
            def one(k, carry):
                t = 4 * j + k
                slot = lax.rem(t, 2)
                wait(loads(t))
                ge[j] = ge[j] + _dot(gbuf[slot], hbuf[slot], 0, 0)

                @pl.when(t + 2 < 16)
                def _():
                    start(loads(t + 2))

                return carry

            ge[j] = jnp.zeros((wx, d), F32)
            lax.fori_loop(0, 4, one, 0)
            send([_Copy(c_copy, j)])

        start(loads(0))
        start(loads(1))
        first_end(0)
        chunk(0)
        second_relay(0)
        chunk(1)
        core_end(0)
        send([_Copy(rx_copy, 0, s) for s in PAIR])
        wait(own_copies)
        gw, back = second_end(0)
        chunk(2)
        core_end(1)
        send([_Copy(rx_copy, 1, 0)])
        back = gather2(0, back)
        chunk(3)
        core_end(2)
        send([_Copy(rx_copy, 1, 1)])
        core_end(3)
        backs.append(back)
        return gw

    half_tile = pltpu.VMEM((len(chunks), rb, LANES), F32)
    tile = pltpu.VMEM((rb, LANES), F32)
    pl.run_scoped(
        logits_stage, pltpu.VMEM((2, rb, v_pad), F32), pltpu.VMEM((2, rb, mw), F32),
        pltpu.VMEM((2, rb, d), F32), pltpu.VMEM((2, rb, d), BF16), pltpu.VMEM((2, rb, d), BF16),
        half_tile, half_tile, tile)
    pl.run_scoped(
        gradient_stage, pltpu.VMEM((2, rb, v_pad), F32), pltpu.VMEM((2, rb, mw), F32),
        pltpu.VMEM((rb, v_pad), BF16), pltpu.VMEM((rb, v_pad), BF16),
        half_tile)
    backs = []
    gw0 = pl.run_scoped(embed_stage, pltpu.VMEM((2, n_tok // 4, wx), BF16), pltpu.VMEM((2, n_tok // 4, d), BF16))

    for s in PAIR:
        rx_copy(0, s).wait_recv()
        j, rows = rows_x(2, s)
        ge[j, rows, mine] = ge[j, rows, mine] + rx[s, 0]
        send([_Copy(rx_copy, 2, s)])
    back0 = gather1_start(0, backs[0])
    first_end(1)
    second_relay(1)
    last0 = gather1(0, back0)
    gw1, back1 = second_end(1)

    row8 = lax.broadcasted_iota(jnp.int32, (8, d), 0)
    small = jnp.where(row8 == 0, gw0 + gw1, jnp.where(row8 == 1, losses[0, 0:1, 0:1] + losses[1, 0:1, 0:1], 0.0))

    def small_start(phase, value):
        place = (y, z, x, core)[phase]
        smb[phase] = value
        smr[phase, place] = value
        devices = ([at_tp(k, 0) for k in OTHERS], [at_tp(0, k) for k in OTHERS], [at_x(k) for k in OTHERS], [partner])[phase]
        return send([_Copy(remote, smb.at[phase], smr.at[phase, place], sm_s.at[phase, k], sm_r.at[phase, k], device)
                     for k, device in enumerate(devices)])

    def small_end(phase, copies):
        recv(copies)
        return functools.reduce(jnp.add, [smr[phase, k] for k in range(2 if phase == 3 else 4)])

    small_step = small_start(0, small)

    def out_rows(k, first=0, size=cx):
        return pl.ds(pl.multiple_of(lax.rem(x + k, 4) * cx + first, 8), size)

    for s in PAIR:
        rx_copy(1, s).wait_recv()
        rx_copy(2, s).wait_recv()
    for half in PAIR:
        j, rows = rows_x(3, half)
        ge[j, rows, mine] = ge[j, rows, mine] + rx[half, 2] + rx[1 - half, 1]
    src = ge.at[3, pl.ds(pl.multiple_of(x_base(3), 8), cx), mine]
    dst = ge_out.at[out_rows(0), mine]
    agx = send([_Copy(remote, src, dst, agx_s.at[s, 0], agx_r.at[s, 0], at_x(STEP[s])) for s in PAIR])
    agc = send([_Copy(remote, src, dst, agc_s.at[0], agc_r.at[0], partner)])
    ge_own = pltpu.make_async_copy(src, dst, out_sem.at[4])
    ge_own.start()
    back1 = gather2(1, back1)
    small_step = small_start(1, small_end(0, small_step))
    back1 = gather1_start(1, back1)
    small_step = small_start(2, small_end(1, small_step))
    fwdx = []
    for s in PAIR:
        agx[s].wait_recv()
        part = ge_out.at[out_rows(STEP[1 - s], s * bx, bx), mine]
        fwdx += send([_Copy(remote, part, part, agx_s.at[s, 1], agx_r.at[s, 1], at_x(STEP[s]))])
        part = ge_out.at[out_rows(STEP[1 - s]), mine]
        agc += send([_Copy(remote, part, part, agc_s.at[1 + s], agc_r.at[1 + s], partner)])
    small_step = small_start(3, small_end(2, small_step))
    small_out[...] = small_end(3, small_step)
    last1 = gather1(1, back1)
    for s in PAIR:
        fwdx[s].wait_recv()
        part = ge_out.at[out_rows(2, s * bx, bx), mine]
        agc += send([_Copy(remote, part, part, agc_s.at[3 + s], agc_r.at[3 + s], partner)])
    recv(last0 + last1)

    for cp in agc:
        cp.wait_recv()
    ge_own.wait()

    def r1_sent(i, carry):
        r1_copy(lax.div(i, 12), lax.rem(lax.div(i, 4), 3), lax.rem(lax.div(i, 2), 2), lax.rem(i, 2)).wait_send()
        return carry

    lax.fori_loop(0, 24, r1_sent, 0)
    for cp in sent:
        cp.wait_send()


def solution(mesh, chunks=(1536, 1664)):
    def program(hidden, residual, targets, embedding, norm_w):
        inv_n = 1.0 / (hidden.shape[0] * hidden.shape[1])
        n_tp = mesh.shape['tp']

        def local_part(hid_loc, res_loc, tgt_loc, emb_loc, norm_vec):
            n_batch, n_seq, d = hid_loc.shape
            n_tok = n_batch * n_seq
            vocab = emb_loc.shape[0]
            v_pad = sum(chunks)
            br = n_tok // 32
            b2 = br // 4
            cx = v_pad // 4
            wx = (cx // LANES + 1) * LANES
            tiles = n_tok // (2 * LANES)
            dma = pltpu.SemaphoreType.DMA
            cube, kinds = (TWO, TWO, TWO), 3
            any_spec = pl.BlockSpec(memory_space=pl.ANY)
            vmem_spec = pl.BlockSpec(memory_space=pltpu.VMEM)
            shape = jax.ShapeDtypeStruct
            gr, ge, small, *_ = pl.pallas_call(
                functools.partial(_kernel, chunks, vocab, inv_n, n_tp),
                grid=(1,),
                in_specs=[vmem_spec, vmem_spec, pl.BlockSpec((16, d), lambda i: (vocab // 16, 0)), any_spec, any_spec, any_spec],
                out_specs=[any_spec, any_spec, vmem_spec, any_spec, any_spec, any_spec, any_spec],
                out_shape=[
                    shape((n_tok, d), F32), shape((v_pad, d), F32), shape((8, d), F32),
                    shape((n_tok, d), BF16), shape((n_tok, v_pad), F32), shape((n_tok, (len(chunks) + 1) * LANES), F32), shape((n_tok, v_pad), BF16),
                ],
                scratch_shapes=[
                    pltpu.VMEM((v_pad, d), BF16),
                    pltpu.VMEM((n_tok, d), F32),
                    pltpu.VMEM((RING, wx, d), F32),
                    pltpu.VMEM(cube + (kinds, br, d), F32),
                    pltpu.VMEM(cube + (kinds, b2, d), F32),
                    pltpu.VMEM((RING, cx, d // TWO), F32),
                    pltpu.VMEM((TWO, kinds, cx // TWO, d // TWO), F32),
                    pltpu.VMEM((TWO, kinds, tiles, LANES), F32),
                    pltpu.VMEM((TWO, RING, kinds, tiles, LANES), F32),
                    pltpu.VMEM((TWO, RING, kinds, tiles, LANES), F32),
                    pltpu.VMEM((TWO, kinds, tiles, LANES), F32),
                    pltpu.VMEM((TWO, TWO * tiles, LANES), F32),
                    pltpu.VMEM((TWO, TWO, TWO * b2, d), F32),
                    pltpu.VMEM((TWO, TWO, TWO * b2, d), BF16),
                    pltpu.VMEM((TWO, 8, LANES), F32),
                    pltpu.VMEM((RING, 8, d), F32),
                    pltpu.VMEM((RING, RING, 8, d), F32),
                    dma, dma(cube), dma(cube), dma(cube), dma(cube), dma((TWO,)), dma((TWO,)), dma(cube),
                ] + [dma((TWO, RING))] * RING + [dma(cube + (kinds,))] * RING + [dma(cube + (TWO,))] * RING + [
                    dma((5,)), dma((RING,)), dma((RING,)), dma((TWO, kinds)), dma((TWO, kinds)), dma((TWO, TWO)), dma((TWO, TWO)),
                    dma((5,)), dma((5,)), dma((RING, kinds)), dma((RING, kinds)),
                ],
                compiler_params=pltpu.CompilerParams(collective_id=0, has_side_effects=True, vmem_limit_bytes=VMEM_BYTES),
                cost_estimate=pl.CostEstimate(flops=6 * n_tok * v_pad * d, bytes_accessed=8 * n_tok * v_pad, transcendentals=0),
            )(tgt_loc.reshape(n_tok // LANES, LANES), norm_vec.reshape(1, d), emb_loc, emb_loc, res_loc.reshape(n_tok, d), hid_loc.reshape(n_tok, d))
            return small[1, 0], gr.reshape(n_batch, n_seq, d), ge[:vocab], small[0]

        sharded = jax.shard_map(
            local_part, mesh=mesh,
            in_specs=(P('dp', None, None), P('dp', None, None), P('dp', None), P('tp', None), P(None)),
            out_specs=(P(), P('dp', None, None), P('tp', None), P(None)),
            check_vma=False)
        return sharded(hidden, residual, targets, embedding, norm_w)

    return program
```

time: 583 us -> 237 us (0.41)
  waiting for transfers between devices: 253 us -> 0 us
  Pallas kernels: 0 us -> 214 us
  blocking collectives: 132 us -> 0 us
  matrix products: 88.9 us -> 0 us
  other arithmetic: 85.4 us -> 0 us
  between operations: 14.8 us -> 0.64 us
  local copies, waits for them, and re-layouts: 8.21 us -> 22.1 us
    psum x2 -> x0, waiting for transfers between devices: 253 us -> none  [the longest x1 171 us: local_part(): lax.psum(jnp.einsum('tv,vd->td', dlogits, emb_loc, preferred_element_type...]
    pallas_call x0 -> x1, Pallas kernels: none -> 214 us  [local_part(): pl.pallas_call(functools.partial(_kernel, chunks, vocab, inv_n, n_tp), gr...]
    dot_general x3 -> x0, matrix products: 88.9 us -> none  [the longest x1 32.1 us: local_part(): jnp.einsum('td,vd->tv', h_act, emb_loc, preferred_element_type=jnp.float32)]
    psum x2 -> x0, blocking collectives: 69.6 us -> none  [the longest x1 55.9 us: local_part(): tok_stats = lax.psum(part_stats, 'tp')]
    pmax x1 -> x0, blocking collectives: 62.5 us -> none  [local_part(): row_max = lax.pmax(jnp.max(logits, axis=-1, keepdims=True), 'tp')]
    reduce_sum x4 -> x0, other arithmetic: 44.7 us -> none  [the longest x1 22.5 us: local_part(): jnp.sum(exp_shift, axis=-1)]
    convert_element_type x1 -> x0, other arithmetic: 26.5 us -> none  [local_part(): (jnp.where(is_target, prob_rows - 1.0, prob_rows) * inv_n).astype(jnp.bfl...]
    reshape x1 -> x0, other arithmetic: 14.2 us -> none  [local_part(): grad_r.reshape(n_batch, n_seq, d_model)]
  transfers between devices with their start and end apart: 2 -> 0, of which waited for: 2 -> 0; matrix products, arithmetic and copies ran while one was open for 9% -> 0% of each run, Pallas kernels for 0% -> 0%
where the time goes in v2:
time: 237 us
  Pallas kernels  214 us (90%)
  local copies, waits for them, and re-layouts  22.1 us (9%)
    pallas_call x1, Pallas kernels, local_part(): pl.pallas_call(functools.partial(_kernel, chunks, vocab, inv_n, n_tp), gr...  214 us
    slice x3, local copies, waits for them, and re-layouts, local_part(): return (small[1, 0], gr.reshape(n_batch, n_seq, d), ge[:vocab], small[0])  10.7 us
    unnamed x1, local copies, waits for them, and re-layouts  10.2 us

profile of v2, /device:TPU:1, one launch (start us, length us, event | category | flops | bytes accessed | tf_op | source)
XLA Modules:
  0.0 237.0 jit_solution(8529288026343411812)
XLA Ops:
  0.6 1.3 reshape.24.w_ref
  1.9 214.2 %shard_map.84 = (f32[4096,768]{1,0:T(8,128)}, f32[3200,768]{1,0:T(8,128)}, f32[8,768]{1,0:T(8,128)}, bf16[4096,768]{1,0:T(8,128)(2,1)}, f32[4096,3200]{1,0:T(8,1...) custom-call(s32[32,128]{1,0:T(8,128)} %bitcast.8, f32[1,768]{1,0:T(1,128)} %reshape.24.w_ref, ...), custom_call_target="tpu_custom_call" | custom-call | flops 60397977600 | bytes 104857600 | tf_op jit(solution)/shard_map/pallas_call | solution.py:685
  216.1 1.2 slice.9
  217.3 1.3 slice_reduce_fusion
  218.6 8.2 %slice.10 = f32[3143,768]{1,0:T(8,128)} slice(f32[3200,768]{1,0:T(8,128)} %get-tuple-element.9), slice={[0:3143], [0:768]} | slice | bytes 19310592 | tf_op jit(solution)/shard_map/slice | solution.py:720
  226.8 10.2 %copy.10 = f32[1,4096,768]{2,1,0:T(8,128)} copy(f32[1,4096,768]{2,1,0:T(8,128)} %bitcast.5) | data formatting | bytes 25165824

commit v3 on v2

--- a/solution.py
+++ b/solution.py
@@ -43,7 +43,7 @@
 def _kernel(chunks, vocab, inv_n, n_tp,
             tgt_ref, w_ref, tail_ref, emb_hbm, res_hbm, hid_hbm,
             gr_out, ge_out, small_out, h_hbm, e_hbm, mc_hbm, g_hbm,
-            emb, dh, ge, r1, r2, crecv, rx, st, sy, sz, st2, fin, rown, hown, losses, smb, smr,
+            emb, dh, ge, r1, r2, crecv, rx, st, sy, sz, st2, fin, rown, hown, losses, gws, smb, smr,
             emb_sem, in_sem, l_sem, e_sem, gw_sem, gin_sem, hin_sem, own_sem, sy_s, sy_r, sz_s, sz_r, r1_s, r1_r, r2_s, r2_r,
             ag2_s, ag2_r, ag1_s, ag1_r, out_sem, c_s, c_r, rx_s, rx_r, agx_s, agx_r, agc_s, agc_r, sm_s, sm_r):
     n_tok, d = dh.shape
@@ -53,6 +53,7 @@
     n_blk = n_tok // rb
     br = n_tok // 32
     b2 = br // 4
+    ck, sb = 2 * br, 2 * b2
     dx = d // 2
     cx = v_pad // 4
     bx = cx // 2
@@ -123,10 +124,10 @@
     own_rows, own_copies = [], []
     for sl in PAIR:
         for c in PAIR:
-            rows = pl.multiple_of(sl * sl_rows + c * (sl_rows // 2) + place1(c) * (2 * br) + place2(c) * (2 * b2), 2 * b2)
+            rows = pl.multiple_of(sl * sl_rows + c * (sl_rows // 2) + place1(c) * ck + place2(c) * sb, sb)
             own_rows.append(rows)
-            own_copies.append(pltpu.make_async_copy(res_hbm.at[pl.ds(rows, 2 * b2), :], rown.at[sl, c], own_sem.at[sl, c, 0]))
-            own_copies.append(pltpu.make_async_copy(hid_hbm.at[pl.ds(rows, 2 * b2), :], hown.at[sl, c], own_sem.at[sl, c, 1]))
+            own_copies.append(pltpu.make_async_copy(res_hbm.at[pl.ds(rows, sb), :], rown.at[sl, c], own_sem.at[sl, c, 0]))
+            own_copies.append(pltpu.make_async_copy(hid_hbm.at[pl.ds(rows, sb), :], hown.at[sl, c], own_sem.at[sl, c, 1]))
 
     def combine(parts):
         top = functools.reduce(jnp.maximum, [p[0] for p in parts])
@@ -278,7 +279,7 @@
         step = 1 + 2 * s
         chunk = lax.rem(place1(c) + jnp.where(kind == 0, 2, jnp.where(kind == 3, 0, step)), 4)
         half = jnp.where(kind == 1, 1 - s, s)
-        return pl.multiple_of(sl * sl_rows + c * (sl_rows // 2) + chunk * (2 * br) + half * br, br)
+        return pl.multiple_of(sl * sl_rows + c * (sl_rows // 2) + chunk * ck + half * br, br)
 
     def r1_copy(sl, kind, c, s):
         rows = pl.ds(rows1(sl, kind, c, s), br)
@@ -375,6 +376,10 @@
             def _():
                 stats_end(1, ahead['z'])
 
+            @pl.when(kk == 6)
+            def _():
+                first_end(0)
+
             step(2 * kk, 0)
             step(2 * kk + 1, 1)
             return carry
@@ -393,7 +398,7 @@
     def rows2(sl, kind, c, s):
         chunk = lax.rem(place2(c) + (2 if kind == 0 else 0 if kind == 3 else STEP[s]), 4)
         half = 1 - s if kind == 1 else s
-        return pl.multiple_of(sl * sl_rows + c * (sl_rows // 2) + place1(c) * (2 * br) + chunk * (2 * b2) + half * b2, b2)
+        return pl.multiple_of(sl * sl_rows + c * (sl_rows // 2) + place1(c) * ck + chunk * sb + half * b2, b2)
 
     def r2_copy(sl, kind, c, s):
         rows = pl.ds(rows2(sl, kind, c, s), b2)
@@ -419,13 +424,14 @@
                 send([_Copy(r2_copy, sl, 2, c, s)])
 
     out_copies = []
+    held = {}
 
     def ag2_copy(sl, c, s):
-        at = pl.ds(own_rows[2 * sl + c], 2 * b2)
+        at = pl.ds(own_rows[2 * sl + c], sb)
         return remote(dh.at[at, :], gr_out.at[at, :], ag2_s.at[sl, c, s, 0], ag2_r.at[sl, c, s, 0], axis2(c, STEP[s]))
 
     def own_copy(sl, c):
-        at = pl.ds(own_rows[2 * sl + c], 2 * b2)
+        at = pl.ds(own_rows[2 * sl + c], sb)
         return pltpu.make_async_copy(dh.at[at, :], gr_out.at[at, :], out_sem.at[2 * sl + c])
 
     def second_end(sl):
@@ -450,13 +456,14 @@
             copies += send([_Copy(ag2_copy, sl, c, s) for s in PAIR])
             out_copies.append(_Copy(own_copy, sl, c))
             out_copies[-1].start()
-        return gw, copies
+        gws[sl] = jnp.broadcast_to(gw, (8, d))
+        return copies
 
     def own_chunk(sl, c, k):
-        return pl.multiple_of(sl * sl_rows + c * (sl_rows // 2) + lax.rem(place1(c) + k, 4) * (2 * br), 2 * br)
+        return pl.multiple_of(sl * sl_rows + c * (sl_rows // 2) + lax.rem(place1(c) + k, 4) * ck, ck)
 
     def fwd2_copy(sl, c, s):
-        rows = pl.multiple_of(own_chunk(sl, c, 0) + lax.rem(place2(c) + STEP[1 - s], 4) * (2 * b2) + s * b2, b2)
+        rows = pl.multiple_of(own_chunk(sl, c, 0) + lax.rem(place2(c) + STEP[1 - s], 4) * sb + s * b2, b2)
         part = gr_out.at[pl.ds(rows, b2), :]
         return remote(part, part, ag2_s.at[sl, c, s, 1], ag2_r.at[sl, c, s, 1], axis2(c, STEP[s]))
 
@@ -469,7 +476,7 @@
         return out
 
     def ag1_copy(sl, c, s):
-        part = gr_out.at[pl.ds(own_chunk(sl, c, 0), 2 * br), :]
+        part = gr_out.at[pl.ds(own_chunk(sl, c, 0), ck), :]
         return remote(part, part, ag1_s.at[sl, c, s, 0], ag1_r.at[sl, c, s, 0], axis1(c, STEP[s]))
 
     def gather1_start(sl, copies):
@@ -535,8 +542,9 @@
             return (pltpu.make_async_copy(g_hbm.at[rows, cols], gbuf.at[slot], gin_sem.at[slot]),
                     pltpu.make_async_copy(h_hbm.at[rows, :], hbuf.at[slot], hin_sem.at[slot]))
 
-        def chunk(j):
+        def chunk(j, middle):
             def one(k, carry):
+                pl.when(k == 2)(middle)
                 t = 4 * j + k
                 slot = lax.rem(t, 2)
                 wait(loads(t))
@@ -552,26 +560,37 @@
             lax.fori_loop(0, 4, one, 0)
             send([_Copy(c_copy, j)])
 
+        def middle1():
+            core_end(0)
+            send([_Copy(rx_copy, 0, s) for s in PAIR])
+            held[0] = second_end(0)
+
+        def middle2():
+            core_end(1)
+            send([_Copy(rx_copy, 1, 0)])
+            second_relay(1)
+            held[0] = gather1_start(0, held[0])
+
+        def middle3():
+            core_end(2)
+            send([_Copy(rx_copy, 1, 1)])
+            for s in PAIR:
+                rx_copy(0, s).wait_recv()
+                j, rows = rows_x(2, s)
+                ge[j, rows, mine] = ge[j, rows, mine] + rx[s, 0]
+                send([_Copy(rx_copy, 2, s)])
+
         start(loads(0))
         start(loads(1))
-        first_end(0)
-        chunk(0)
-        second_relay(0)
-        chunk(1)
-        core_end(0)
-        send([_Copy(rx_copy, 0, s) for s in PAIR])
         wait(own_copies)
-        gw, back = second_end(0)
-        chunk(2)
-        core_end(1)
-        send([_Copy(rx_copy, 1, 0)])
-        back = gather2(0, back)
-        chunk(3)
-        core_end(2)
-        send([_Copy(rx_copy, 1, 1)])
+        chunk(0, functools.partial(second_relay, 0))
+        chunk(1, middle1)
+        held[0] = gather2(0, held[0])
+        first_end(1)
+        chunk(2, middle2)
+        held[1] = second_end(1)
+        chunk(3, middle3)
         core_end(3)
-        backs.append(back)
-        return gw
 
     half_tile = pltpu.VMEM((len(chunks), rb, LANES), F32)
     tile = pltpu.VMEM((rb, LANES), F32)
@@ -583,22 +602,10 @@
         gradient_stage, pltpu.VMEM((2, rb, v_pad), F32), pltpu.VMEM((2, rb, mw), F32),
         pltpu.VMEM((rb, v_pad), BF16), pltpu.VMEM((rb, v_pad), BF16),
         half_tile)
-    backs = []
-    gw0 = pl.run_scoped(embed_stage, pltpu.VMEM((2, n_tok // 4, wx), BF16), pltpu.VMEM((2, n_tok // 4, d), BF16))
-
-    for s in PAIR:
-        rx_copy(0, s).wait_recv()
-        j, rows = rows_x(2, s)
-        ge[j, rows, mine] = ge[j, rows, mine] + rx[s, 0]
-        send([_Copy(rx_copy, 2, s)])
-    back0 = gather1_start(0, backs[0])
-    first_end(1)
-    second_relay(1)
-    last0 = gather1(0, back0)
-    gw1, back1 = second_end(1)
+    pl.run_scoped(embed_stage, pltpu.VMEM((2, n_tok // 4, wx), BF16), pltpu.VMEM((2, n_tok // 4, d), BF16))
 
     row8 = lax.broadcasted_iota(jnp.int32, (8, d), 0)
-    small = jnp.where(row8 == 0, gw0 + gw1, jnp.where(row8 == 1, losses[0, 0:1, 0:1] + losses[1, 0:1, 0:1], 0.0))
+    small = jnp.where(row8 == 0, gws[0] + gws[1], jnp.where(row8 == 1, losses[0, 0:1, 0:1] + losses[1, 0:1, 0:1], 0.0))
 
     def small_start(phase, value):
         place = (y, z, x, core)[phase]
@@ -613,6 +620,9 @@
         return functools.reduce(jnp.add, [smr[phase, k] for k in range(2 if phase == 3 else 4)])
 
     small_step = small_start(0, small)
+    last0 = gather1(0, held[0])
+    back1 = gather1_start(1, gather2(1, held[1]))
+    small_step = small_start(1, small_end(0, small_step))
 
     def out_rows(k, first=0, size=cx):
         return pl.ds(pl.multiple_of(lax.rem(x + k, 4) * cx + first, 8), size)
@@ -629,10 +639,8 @@
     agc = send([_Copy(remote, src, dst, agc_s.at[0], agc_r.at[0], partner)])
     ge_own = pltpu.make_async_copy(src, dst, out_sem.at[4])
     ge_own.start()
-    back1 = gather2(1, back1)
-    small_step = small_start(1, small_end(0, small_step))
-    back1 = gather1_start(1, back1)
     small_step = small_start(2, small_end(1, small_step))
+    last1 = gather1(1, back1)
     fwdx = []
     for s in PAIR:
         agx[s].wait_recv()
@@ -641,12 +649,11 @@
         part = ge_out.at[out_rows(STEP[1 - s]), mine]
         agc += send([_Copy(remote, part, part, agc_s.at[1 + s], agc_r.at[1 + s], partner)])
     small_step = small_start(3, small_end(2, small_step))
-    small_out[...] = small_end(3, small_step)
-    last1 = gather1(1, back1)
     for s in PAIR:
         fwdx[s].wait_recv()
         part = ge_out.at[out_rows(2, s * bx, bx), mine]
         agc += send([_Copy(remote, part, part, agc_s.at[3 + s], agc_r.at[3 + s], partner)])
+    small_out[...] = small_end(3, small_step)
     recv(last0 + last1)
 
     for cp in agc:
@@ -707,6 +714,7 @@
                     pltpu.VMEM((TWO, TWO, TWO * b2, d), F32),
                     pltpu.VMEM((TWO, TWO, TWO * b2, d), BF16),
                     pltpu.VMEM((TWO, 8, LANES), F32),
+                    pltpu.VMEM((TWO, 8, d), F32),
                     pltpu.VMEM((RING, 8, d), F32),
                     pltpu.VMEM((RING, RING, 8, d), F32),
                     dma, dma(cube), dma(cube), dma(cube), dma(cube), dma((TWO,)), dma((TWO,)), dma(cube),

time: 237 us -> 233 us (0.983)
  Pallas kernels: 214 us -> 210 us
    pallas_call x1, Pallas kernels: 214 us -> 210 us  [local_part(): pl.pallas_call(functools.partial(_kernel, chunks, vocab, inv_n, n_tp), gr...]
where the time goes in v3:
time: 233 us
  Pallas kernels  210 us (90%)
  local copies, waits for them, and re-layouts  22.1 us (9%)
    pallas_call x1, Pallas kernels, local_part(): pl.pallas_call(functools.partial(_kernel, chunks, vocab, inv_n, n_tp), gr...  210 us
    slice x3, local copies, waits for them, and re-layouts, local_part(): return (small[1, 0], gr.reshape(n_batch, n_seq, d), ge[:vocab], small[0])  10.7 us
    unnamed x1, local copies, waits for them, and re-layouts  10.2 us

profile of v3, /device:TPU:1, one launch (start us, length us, event | category | flops | bytes accessed | tf_op | source)
XLA Modules:
  0.0 233.0 jit_solution(14872334205376988442)
XLA Ops:
  0.6 1.3 reshape.24.w_ref
  1.9 210.2 %shard_map.84 = (f32[4096,768]{1,0:T(8,128)}, f32[3200,768]{1,0:T(8,128)}, f32[8,768]{1,0:T(8,128)}, bf16[4096,768]{1,0:T(8,128)(2,1)}, f32[4096,3200]{1,0:T(8,1...) custom-call(s32[32,128]{1,0:T(8,128)} %bitcast.8, f32[1,768]{1,0:T(1,128)} %reshape.24.w_ref, ...), custom_call_target="tpu_custom_call" | custom-call | flops 60397977600 | bytes 104857600 | tf_op jit(solution)/shard_map/pallas_call | solution.py:692
  212.1 1.2 slice.9
  213.3 1.3 slice_reduce_fusion
  214.6 8.2 %slice.10 = f32[3143,768]{1,0:T(8,128)} slice(f32[3200,768]{1,0:T(8,128)} %get-tuple-element.9), slice={[0:3143], [0:768]} | slice | bytes 19310592 | tf_op jit(solution)/shard_map/slice | solution.py:728
  222.8 10.2 %copy.10 = f32[1,4096,768]{2,1,0:T(8,128)} copy(f32[1,4096,768]{2,1,0:T(8,128)} %bitcast.5) | data formatting | bytes 25165824

commit v4 on v3

--- a/solution.py
+++ b/solution.py
@@ -532,6 +532,20 @@
         j, rows = rows_x(kind, s)
         return remote(ge.at[j, rows, mine], rx.at[s, kind], rx_s.at[s, kind], rx_r.at[s, kind], at_x(STEP[s]))
 
+    def small_copy(phase, k):
+        place = (y, z, x, core)[phase]
+        device = (at_tp(k, 0), at_tp(0, k), at_x(k), partner)[phase]
+        return remote(smb.at[phase], smr.at[phase, place], sm_s.at[phase, k - 1], sm_r.at[phase, k - 1], device)
+
+    def small_start(phase, value):
+        smb[phase] = value
+        smr[phase, (y, z, x, core)[phase]] = value
+        return send([_Copy(small_copy, phase, k) for k in (OTHERS[:1] if phase == 3 else OTHERS)])
+
+    def small_end(phase, copies):
+        recv(copies)
+        return functools.reduce(jnp.add, [smr[phase, k] for k in (PAIR if phase == 3 else range(RING))])
+
     def embed_stage(gbuf, hbuf):
         kb = n_tok // 4
 
@@ -569,7 +583,6 @@
             core_end(1)
             send([_Copy(rx_copy, 1, 0)])
             second_relay(1)
-            held[0] = gather1_start(0, held[0])
 
         def middle3():
             core_end(2)
@@ -579,6 +592,8 @@
                 j, rows = rows_x(2, s)
                 ge[j, rows, mine] = ge[j, rows, mine] + rx[s, 0]
                 send([_Copy(rx_copy, 2, s)])
+            held[1] = gather2(1, held[1])
+            held['small'] = small_start(1, small_end(0, held['small']))
 
         start(loads(0))
         start(loads(1))
@@ -589,6 +604,9 @@
         first_end(1)
         chunk(2, middle2)
         held[1] = second_end(1)
+        row8 = lax.broadcasted_iota(jnp.int32, (8, d), 0)
+        loss = losses[0, 0:1, 0:1] + losses[1, 0:1, 0:1]
+        held['small'] = small_start(0, jnp.where(row8 == 0, gws[0] + gws[1], jnp.where(row8 == 1, loss, 0.0)))
         chunk(3, middle3)
         core_end(3)
 
@@ -604,25 +622,9 @@
         half_tile)
     pl.run_scoped(embed_stage, pltpu.VMEM((2, n_tok // 4, wx), BF16), pltpu.VMEM((2, n_tok // 4, d), BF16))
 
-    row8 = lax.broadcasted_iota(jnp.int32, (8, d), 0)
-    small = jnp.where(row8 == 0, gws[0] + gws[1], jnp.where(row8 == 1, losses[0, 0:1, 0:1] + losses[1, 0:1, 0:1], 0.0))
-
-    def small_start(phase, value):
-        place = (y, z, x, core)[phase]
-        smb[phase] = value
-        smr[phase, place] = value
-        devices = ([at_tp(k, 0) for k in OTHERS], [at_tp(0, k) for k in OTHERS], [at_x(k) for k in OTHERS], [partner])[phase]
-        return send([_Copy(remote, smb.at[phase], smr.at[phase, place], sm_s.at[phase, k], sm_r.at[phase, k], device)
-                     for k, device in enumerate(devices)])
-
-    def small_end(phase, copies):
-        recv(copies)
-        return functools.reduce(jnp.add, [smr[phase, k] for k in range(2 if phase == 3 else 4)])
-
-    small_step = small_start(0, small)
-    last0 = gather1(0, held[0])
-    back1 = gather1_start(1, gather2(1, held[1]))
-    small_step = small_start(1, small_end(0, small_step))
+    held['small'] = small_start(2, small_end(1, held['small']))
+    back0 = gather1_start(0, held[0])
+    back1 = gather1_start(1, held[1])
 
     def out_rows(k, first=0, size=cx):
         return pl.ds(pl.multiple_of(lax.rem(x + k, 4) * cx + first, 8), size)
@@ -639,7 +641,8 @@
     agc = send([_Copy(remote, src, dst, agc_s.at[0], agc_r.at[0], partner)])
     ge_own = pltpu.make_async_copy(src, dst, out_sem.at[4])
     ge_own.start()
-    small_step = small_start(2, small_end(1, small_step))
+    last0 = gather1(0, back0)
+    held['small'] = small_start(3, small_end(2, held['small']))
     last1 = gather1(1, back1)
     fwdx = []
     for s in PAIR:
@@ -648,12 +651,11 @@
         fwdx += send([_Copy(remote, part, part, agx_s.at[s, 1], agx_r.at[s, 1], at_x(STEP[s]))])
         part = ge_out.at[out_rows(STEP[1 - s]), mine]
         agc += send([_Copy(remote, part, part, agc_s.at[1 + s], agc_r.at[1 + s], partner)])
-    small_step = small_start(3, small_end(2, small_step))
     for s in PAIR:
         fwdx[s].wait_recv()
         part = ge_out.at[out_rows(2, s * bx, bx), mine]
         agc += send([_Copy(remote, part, part, agc_s.at[3 + s], agc_r.at[3 + s], partner)])
-    small_out[...] = small_end(3, small_step)
+    small_out[...] = small_end(3, held['small'])
     recv(last0 + last1)
 
     for cp in agc:

time: 233 us -> 231 us (level)
  Pallas kernels: 210 us -> 207 us
    pallas_call x1, Pallas kernels: 210 us -> 207 us  [local_part(): pl.pallas_call(functools.partial(_kernel, chunks, vocab, inv_n, n_tp), gr...]
where the time goes in v4:
time: 231 us; the launch traced here: 230 us
  Pallas kernels  207 us (90%)
  local copies, waits for them, and re-layouts  22.1 us (10%)
    pallas_call x1, Pallas kernels, local_part(): pl.pallas_call(functools.partial(_kernel, chunks, vocab, inv_n, n_tp), gr...  207 us
    slice x3, local copies, waits for them, and re-layouts, local_part(): return (small[1, 0], gr.reshape(n_batch, n_seq, d), ge[:vocab], small[0])  10.7 us
    unnamed x1, local copies, waits for them, and re-layouts  10.2 us

profile of v4, /device:TPU:1, one launch (start us, length us, event | category | flops | bytes accessed | tf_op | source)
XLA Modules:
  0.0 229.8 jit_solution(2106828331250691465)
XLA Ops:
  0.6 1.3 reshape.24.w_ref
  1.9 207.1 %shard_map.84 = (f32[4096,768]{1,0:T(8,128)}, f32[3200,768]{1,0:T(8,128)}, f32[8,768]{1,0:T(8,128)}, bf16[4096,768]{1,0:T(8,128)(2,1)}, f32[4096,3200]{1,0:T(8,1...) custom-call(s32[32,128]{1,0:T(8,128)} %bitcast.8, f32[1,768]{1,0:T(1,128)} %reshape.24.w_ref, ...), custom_call_target="tpu_custom_call" | custom-call | flops 60397977600 | bytes 104857600 | tf_op jit(solution)/shard_map/pallas_call | solution.py:694
  209.0 1.2 slice.9
  210.2 1.3 slice_reduce_fusion
  211.5 8.2 %slice.10 = f32[3143,768]{1,0:T(8,128)} slice(f32[3200,768]{1,0:T(8,128)} %get-tuple-element.9), slice={[0:3143], [0:768]} | slice | bytes 19310592 | tf_op jit(solution)/shard_map/slice | solution.py:730
  219.7 10.2 %copy.10 = f32[1,4096,768]{2,1,0:T(8,128)} copy(f32[1,4096,768]{2,1,0:T(8,128)} %bitcast.5) | data formatting | bytes 25165824

commit v5 on v4

--- a/solution.py
+++ b/solution.py
@@ -558,7 +558,8 @@
 
         def chunk(j, middle):
             def one(k, carry):
-                pl.when(k == 2)(middle)
+                if middle:
+                    pl.when(k == 2)(middle)
                 t = 4 * j + k
                 slot = lax.rem(t, 2)
                 wait(loads(t))
@@ -577,12 +578,11 @@
         def middle1():
             core_end(0)
             send([_Copy(rx_copy, 0, s) for s in PAIR])
-            held[0] = second_end(0)
 
         def middle2():
             core_end(1)
             send([_Copy(rx_copy, 1, 0)])
-            second_relay(1)
+            held[0] = gather2(0, held[0])
 
         def middle3():
             core_end(2)
@@ -592,21 +592,21 @@
                 j, rows = rows_x(2, s)
                 ge[j, rows, mine] = ge[j, rows, mine] + rx[s, 0]
                 send([_Copy(rx_copy, 2, s)])
-            held[1] = gather2(1, held[1])
-            held['small'] = small_start(1, small_end(0, held['small']))
+            held[1] = second_end(1)
+            row8 = lax.broadcasted_iota(jnp.int32, (8, d), 0)
+            loss = losses[0, 0:1, 0:1] + losses[1, 0:1, 0:1]
+            held['small'] = small_start(0, jnp.where(row8 == 0, gws[0] + gws[1], jnp.where(row8 == 1, loss, 0.0)))
 
         start(loads(0))
         start(loads(1))
         wait(own_copies)
-        chunk(0, functools.partial(second_relay, 0))
+        chunk(0, None)
+        second_relay(0)
         chunk(1, middle1)
-        held[0] = gather2(0, held[0])
+        held[0] = second_end(0)
         first_end(1)
         chunk(2, middle2)
-        held[1] = second_end(1)
-        row8 = lax.broadcasted_iota(jnp.int32, (8, d), 0)
-        loss = losses[0, 0:1, 0:1] + losses[1, 0:1, 0:1]
-        held['small'] = small_start(0, jnp.where(row8 == 0, gws[0] + gws[1], jnp.where(row8 == 1, loss, 0.0)))
+        second_relay(1)
         chunk(3, middle3)
         core_end(3)
 
@@ -622,8 +622,10 @@
         half_tile)
     pl.run_scoped(embed_stage, pltpu.VMEM((2, n_tok // 4, wx), BF16), pltpu.VMEM((2, n_tok // 4, d), BF16))
 
+    held[1] = gather2(1, held[1])
+    held['small'] = small_start(1, small_end(0, held['small']))
+    back0 = gather1_start(0, held[0])
     held['small'] = small_start(2, small_end(1, held['small']))
-    back0 = gather1_start(0, held[0])
     back1 = gather1_start(1, held[1])
 
     def out_rows(k, first=0, size=cx):
@@ -635,9 +637,14 @@
     for half in PAIR:
         j, rows = rows_x(3, half)
         ge[j, rows, mine] = ge[j, rows, mine] + rx[half, 2] + rx[1 - half, 1]
+    def agx_copy(s, late):
+        _, rows = rows_x(3, 1 - s if late else s)
+        dst = ge_out.at[out_rows(0, (1 - s if late else s) * bx, bx), mine]
+        return remote(ge.at[3, rows, mine], dst, agx_s.at[s, late], agx_r.at[s, late], at_x(STEP[s]))
+
+    agx, agx_late = (send([_Copy(agx_copy, s, late) for s in PAIR]) for late in PAIR)
     src = ge.at[3, pl.ds(pl.multiple_of(x_base(3), 8), cx), mine]
     dst = ge_out.at[out_rows(0), mine]
-    agx = send([_Copy(remote, src, dst, agx_s.at[s, 0], agx_r.at[s, 0], at_x(STEP[s])) for s in PAIR])
     agc = send([_Copy(remote, src, dst, agc_s.at[0], agc_r.at[0], partner)])
     ge_own = pltpu.make_async_copy(src, dst, out_sem.at[4])
     ge_own.start()
@@ -648,7 +655,9 @@
     for s in PAIR:
         agx[s].wait_recv()
         part = ge_out.at[out_rows(STEP[1 - s], s * bx, bx), mine]
-        fwdx += send([_Copy(remote, part, part, agx_s.at[s, 1], agx_r.at[s, 1], at_x(STEP[s]))])
+        fwdx += send([_Copy(remote, part, part, agx_s.at[s, TWO], agx_r.at[s, TWO], at_x(STEP[s]))])
+    for s in PAIR:
+        agx_late[s].wait_recv()
         part = ge_out.at[out_rows(STEP[1 - s]), mine]
         agc += send([_Copy(remote, part, part, agc_s.at[1 + s], agc_r.at[1 + s], partner)])
     for s in PAIR:
@@ -721,7 +730,7 @@
                     pltpu.VMEM((RING, RING, 8, d), F32),
                     dma, dma(cube), dma(cube), dma(cube), dma(cube), dma((TWO,)), dma((TWO,)), dma(cube),
                 ] + [dma((TWO, RING))] * RING + [dma(cube + (kinds,))] * RING + [dma(cube + (TWO,))] * RING + [
-                    dma((5,)), dma((RING,)), dma((RING,)), dma((TWO, kinds)), dma((TWO, kinds)), dma((TWO, TWO)), dma((TWO, TWO)),
+                    dma((5,)), dma((RING,)), dma((RING,)), dma((TWO, kinds)), dma((TWO, kinds)), dma((TWO, kinds)), dma((TWO, kinds)),
                     dma((5,)), dma((5,)), dma((RING, kinds)), dma((RING, kinds)),
                 ],
                 compiler_params=pltpu.CompilerParams(collective_id=0, has_side_effects=True, vmem_limit_bytes=VMEM_BYTES),

time: 231 us -> 228 us (0.987)
  Pallas kernels: 207 us -> 204 us
    pallas_call x1, Pallas kernels: 207 us -> 204 us  [local_part(): pl.pallas_call(functools.partial(_kernel, chunks, vocab, inv_n, n_tp), gr...]
where the time goes in v5:
time: 228 us; the launch traced here: 227 us
  Pallas kernels  204 us (89%)
  local copies, waits for them, and re-layouts  22.1 us (10%)
    pallas_call x1, Pallas kernels, local_part(): pl.pallas_call(functools.partial(_kernel, chunks, vocab, inv_n, n_tp), gr...  204 us
    slice x3, local copies, waits for them, and re-layouts, local_part(): return (small[1, 0], gr.reshape(n_batch, n_seq, d), ge[:vocab], small[0])  10.7 us
    unnamed x1, local copies, waits for them, and re-layouts  10.2 us

profile of v5, /device:TPU:1, one launch (start us, length us, event | category | flops | bytes accessed | tf_op | source)
XLA Modules:
  0.0 227.2 jit_solution(14855899865662855494)
XLA Ops:
  0.6 1.3 reshape.24.w_ref
  1.9 204.4 %shard_map.84 = (f32[4096,768]{1,0:T(8,128)}, f32[3200,768]{1,0:T(8,128)}, f32[8,768]{1,0:T(8,128)}, bf16[4096,768]{1,0:T(8,128)(2,1)}, f32[4096,3200]{1,0:T(8,1...) custom-call(s32[32,128]{1,0:T(8,128)} %bitcast.8, f32[1,768]{1,0:T(1,128)} %reshape.24.w_ref, ...), custom_call_target="tpu_custom_call" | custom-call | flops 60397977600 | bytes 104857600 | tf_op jit(solution)/shard_map/pallas_call | solution.py:703
  206.3 1.2 slice.9
  207.5 1.3 slice_reduce_fusion
  208.8 8.2 %slice.10 = f32[3143,768]{1,0:T(8,128)} slice(f32[3200,768]{1,0:T(8,128)} %get-tuple-element.9), slice={[0:3143], [0:768]} | slice | bytes 19310592 | tf_op jit(solution)/shard_map/slice | solution.py:739
  217.0 10.2 %copy.10 = f32[1,4096,768]{2,1,0:T(8,128)} copy(f32[1,4096,768]{2,1,0:T(8,128)} %bitcast.5) | data formatting | bytes 25165824
